TPU v7x, 32 devices: a whole 2x2x4 slice. The times are simulated.
32 devices in a mesh: dp: 4 (over y, x), tensor: 8 (over z, core).
Axes of the slice: x: 2, y: 2, z: 4, core: 2. Of those that a mesh axis runs over, the one named last changes fastest.
Arguments:
- noisy: bfloat16 [32, 256, 1152], P('dp', None, 'tensor'), may hold values from -6 to 6
- labels: int32 [32], P('dp'), may hold values from 0 to 999
- tsteps: int32 [32], P('dp'), may hold values from 0 to 999
- guide_index: int32 [32], P('dp'), may hold values from 0 to 31
- class_table: bfloat16 [1001, 1152], replicated, may hold values from -6 to 6
- time_table: bfloat16 [1000, 1152], replicated, may hold values from -6 to 6
- guide_table: bfloat16 [32, 1152], replicated, may hold values from -6 to 6
- guide_weights: float32 [32], replicated, may hold values from 0.5 to 4
- teacher_qkv: bfloat16 [1152, 3456], P(None, 'tensor'), may hold values from -0.1875 to 0.1875
- teacher_out: bfloat16 [1152, 1152], P('tensor'), may hold values from -0.1875 to 0.1875
- teacher_ada: bfloat16 [3, 1152, 1152], P(None, None, 'tensor'), may hold values from -0.1875 to 0.1875
- student_qkv: bfloat16 [1152, 3456], P(None, 'tensor'), may hold values from -0.1875 to 0.1875
- student_out: bfloat16 [1152, 1152], P('tensor'), may hold values from -0.1875 to 0.1875
- student_ada: bfloat16 [3, 1152, 1152], P(None, None, 'tensor'), may hold values from -0.1875 to 0.1875
Outputs:
- grad_qkv: float32 [1152, 3456], P('dp', 'tensor')
- grad_out: float32 [1152, 1152], P('tensor', 'dp')
- grad_ada: float32 [3, 1152, 1152], P(None, 'dp', 'tensor')
All inputs are finite; a program needn't handle non-finite values.
Results may differ from a plain program's by a relative error of at most 0.034.
Values may be sent and summed in bfloat16 or wider, within the bound.
A program may use at most 128 MiB of HBM per device.

v0:
```python
import math

import jax
import jax.numpy as jnp
from jax import lax
from jax.sharding import PartitionSpec as P

HD = 72


norm_eps = 1e-06


def lookup_rows(indices, table_rows):
    one_hot = (
        indices[:, None] == jnp.arange(table_rows.shape[0], dtype=jnp.int32)[None, :]
    ).astype(table_rows.dtype)
    return jnp.dot(one_hot, table_rows, preferred_element_type=jnp.float32)


def attend(qkv_sums, heads_here):
    batch_rows, seq_len = (qkv_sums.shape[0], qkv_sums.shape[1])
    heads_qkv = qkv_sums.astype(jnp.bfloat16).reshape(batch_rows, seq_len, heads_here, 3, HD)
    queries, key_rows, values = (
        heads_qkv[:, :, :, 0],
        heads_qkv[:, :, :, 1],
        heads_qkv[:, :, :, 2],
    )
    scores = jnp.einsum(
        "blhe,bmhe->bhlm", queries, key_rows, preferred_element_type=jnp.float32
    ) * (1.0 / math.sqrt(HD))
    exponent = jnp.exp(scores - jnp.max(scores, axis=-1, keepdims=True))
    attn_prob = exponent / jnp.sum(exponent, axis=-1, keepdims=True)
    prob_low = attn_prob.astype(jnp.bfloat16)
    attn_mixed = jnp.einsum("bhlm,bmhe->blhe", prob_low, values, preferred_element_type=jnp.float32)
    attn_mixed = attn_mixed.astype(jnp.bfloat16).reshape(batch_rows, seq_len, heads_here * HD)
    return (heads_qkv, attn_prob, prob_low, attn_mixed)


def attend_grad(heads_qkv, attn_prob, prob_low, grad_low):
    batch_rows, seq_len = (heads_qkv.shape[0], heads_qkv.shape[1])
    queries, key_rows, values = (
        heads_qkv[:, :, :, 0],
        heads_qkv[:, :, :, 1],
        heads_qkv[:, :, :, 2],
    )
    grad_probs = jnp.einsum("blhe,bmhe->bhlm", grad_low, values, preferred_element_type=jnp.float32)
    row_delta = jnp.sum(attn_prob * grad_probs, axis=-1, keepdims=True)
    grad_scores = (attn_prob * (grad_probs - row_delta) * (1.0 / math.sqrt(HD))).astype(
        jnp.bfloat16
    )
    grad_query = jnp.einsum(
        "bhlm,bmhe->blhe", grad_scores, key_rows, preferred_element_type=jnp.float32
    )
    grad_keys = jnp.einsum(
        "bhlm,blhe->bmhe", grad_scores, queries, preferred_element_type=jnp.float32
    )
    grad_values = jnp.einsum(
        "bhlm,blhe->bmhe", prob_low, grad_low, preferred_element_type=jnp.float32
    )
    grad_qkv_act = jnp.stack([grad_query, grad_keys, grad_values], axis=3).astype(jnp.bfloat16)
    return grad_qkv_act.reshape(batch_rows, seq_len, -1)


def forward(source, embed_act, qkv_weight, out_weight, ada_weight):
    heads_here = out_weight.shape[0] // HD
    modulation = jnp.einsum(
        "bd,kde->bke", embed_act, ada_weight, preferred_element_type=jnp.float32
    )
    wide_mod = lax.all_gather(modulation, "tensor", axis=2, tiled=True)
    full_rows = (
        source.astype(jnp.float32) * (1.0 + wide_mod[:, 1][:, None]) + wide_mod[:, 0][:, None]
    ).astype(jnp.bfloat16)
    qkv_sums = jnp.einsum("bld,df->blf", full_rows, qkv_weight, preferred_element_type=jnp.float32)
    heads_qkv, attn_prob, prob_low, attn_mixed = attend(qkv_sums, heads_here)
    partial_value = jnp.einsum(
        "blf,fd->bld", attn_mixed, out_weight, preferred_element_type=jnp.float32
    )
    projected = lax.psum_scatter(
        partial_value.astype(jnp.bfloat16), "tensor", scatter_dimension=2, tiled=True
    ).astype(jnp.float32)
    branch = modulation[:, 2][:, None] * projected
    return (branch, (full_rows, heads_qkv, attn_prob, prob_low, attn_mixed, projected, modulation))


def local(
    noisy,
    labels,
    tsteps,
    guide_index,
    class_table,
    time_table,
    guide_table,
    guide_weights,
    teacher_qkv,
    teacher_out,
    teacher_ada,
    student_qkv,
    student_out,
    student_ada,
):
    samples, seq_len, width_part = noisy.shape
    model_width = width_part * lax.axis_size("tensor")
    batch_size = samples * lax.axis_size("dp")
    signal = noisy.astype(jnp.float32)
    row_sums = lax.psum((jnp.sum(signal, axis=2), jnp.sum(signal * signal, axis=2)), "tensor")
    row_mean = row_sums[0] / model_width
    row_var = row_sums[1] / model_width - row_mean * row_mean
    normed = ((signal - row_mean[:, :, None]) * lax.rsqrt(row_var + norm_eps)[:, :, None]).astype(
        jnp.bfloat16
    )
    null_class = class_table.shape[0] - 1
    time_embed = lookup_rows(tsteps, time_table)
    cond_embed = lookup_rows(labels, class_table) + time_embed
    null_embed = class_table[null_class].astype(jnp.float32)[None, :] + time_embed
    guide_hot = guide_index[:, None] == jnp.arange(guide_table.shape[0], dtype=jnp.int32)[None, :]
    student_embed = cond_embed + jnp.dot(
        guide_hot.astype(jnp.bfloat16), guide_table, preferred_element_type=jnp.float32
    )
    strength = jnp.sum(jnp.where(guide_hot, guide_weights[None, :], 0.0), axis=1)
    cond_act = jax.nn.silu(cond_embed).astype(jnp.bfloat16)
    null_act = jax.nn.silu(null_embed).astype(jnp.bfloat16)
    student_act = jax.nn.silu(student_embed).astype(jnp.bfloat16)
    scale_norm = 1.0 / math.sqrt(batch_size * seq_len)
    wide_rows = lax.all_gather(normed, "tensor", axis=2, tiled=True)
    teacher_full = jnp.concatenate([wide_rows, wide_rows], axis=0)
    teacher_act = jnp.concatenate([cond_act, null_act], axis=0)
    teacher_branch, unused_saved = forward(
        teacher_full, teacher_act, teacher_qkv, teacher_out, teacher_ada
    )
    teacher_update = teacher_branch.astype(jnp.bfloat16).astype(jnp.float32)
    scaled = strength[:, None, None]
    target = signal + (
        (1.0 + scaled) * teacher_update[:samples] - scaled * teacher_update[samples:]
    )
    branch, saved = forward(wide_rows, student_act, student_qkv, student_out, student_ada)
    full_rows, heads_qkv, attn_prob, prob_low, attn_mixed, projected, modulation = saved
    heads_here = student_out.shape[0] // HD
    cotangent = (signal + branch - target) * scale_norm
    grad_gate = jnp.sum(cotangent * projected, axis=1)
    grad_proj = (cotangent * modulation[:, 2][:, None]).astype(jnp.bfloat16)
    gathered = lax.all_gather(grad_proj, "tensor", axis=2, tiled=True)
    grad_mixed = jnp.einsum(
        "bld,ed->ble", gathered, student_out, preferred_element_type=jnp.float32
    )
    block_grad = jnp.einsum("ble,bld->ed", attn_mixed, gathered, preferred_element_type=jnp.float32)
    grad_mixed, grad_out_rows = (grad_mixed, block_grad)
    grad_low = grad_mixed.astype(jnp.bfloat16).reshape(samples, seq_len, heads_here, HD)
    grad_qkv_act = attend_grad(heads_qkv, attn_prob, prob_low, grad_low)
    grad_qkv_local = jnp.einsum(
        "bld,blf->df", full_rows, grad_qkv_act, preferred_element_type=jnp.float32
    )
    input_terms = jnp.einsum(
        "blf,df->bld", grad_qkv_act, student_qkv, preferred_element_type=jnp.float32
    )
    grad_input = lax.psum_scatter(
        input_terms.astype(jnp.bfloat16), "tensor", scatter_dimension=2, tiled=True
    ).astype(jnp.float32)
    grad_shift = jnp.sum(grad_input, axis=1)
    grad_scale = jnp.sum(grad_input * normed.astype(jnp.float32), axis=1)
    grad_modulation = jnp.stack([grad_shift, grad_scale, grad_gate], axis=1)
    grad_ada_local = jnp.einsum(
        "bd,bke->kde",
        student_act.astype(jnp.float32),
        grad_modulation,
        precision=lax.Precision.HIGHEST,
    )
    grad_qkv, grad_out, grad_ada = (
        lax.psum_scatter(
            grad_qkv_local.astype(jnp.bfloat16), "dp", scatter_dimension=0, tiled=True
        ).astype(jnp.float32),
        lax.psum_scatter(
            grad_out_rows.astype(jnp.bfloat16), "dp", scatter_dimension=1, tiled=True
        ).astype(jnp.float32),
        lax.psum_scatter(
            grad_ada_local.astype(jnp.bfloat16), "dp", scatter_dimension=1, tiled=True
        ).astype(jnp.float32),
    )
    return (grad_qkv, grad_out, grad_ada)


def solution(mesh):
    return jax.shard_map(
        local,
        mesh=mesh,
        in_specs=(
            P("dp", None, "tensor"),
            P("dp"),
            P("dp"),
            P("dp"),
            P(),
            P(),
            P(),
            P(),
            P(None, "tensor"),
            P("tensor", None),
            P(None, None, "tensor"),
            P(None, "tensor"),
            P("tensor", None),
            P(None, None, "tensor"),
        ),
        out_specs=(P("dp", "tensor"), P("tensor", "dp"), P(None, "dp", "tensor")),
        check_vma=False,
    )
```

profile of v0, /device:TPU:0, one launch (start us, length us, event | category | flops | bytes accessed | tf_op | source)
XLA Modules:
  0.0 544.9 jit_solution(2838430340158237559)
XLA Ops:
  7.2 1.4 convert_reduce_fusion
  8.6 30.3 %all-reduce = (f32[8,256]{1,0:T(8,128)S(1)}, f32[8,256]{1,0:T(8,128)S(1)}) all-reduce(f32[8,256]{1,0:T(8,128)S(1)} %get-tuple-element.6, f32[8,256]{1,0:T(8,128)S(1)} %get-tuple-element.5), channel_id=1, replica_groups=mesh['dp'=4,'tensor'=8] {'tensor'}, use_global_device_ids=true, to_apply=%region_3.0 | all-reduce | flops 4096 | bytes 32768 | tf_op jit(solution)/shard_map/psum | solution.py:106
  38.9 2.0 fusion.54
  41.0 0.7 convert_reduce_fusion.2
  41.8 1.1 multiply_convert_fusion.3
  42.9 2.1 multiply_convert_fusion.4
  45.1 0.4 fusion.70
  45.5 0.2 copy.72
  45.7 40.4 %all_gather.14 = f32[16,3,1152]{0,1,2:T(4,128)S(1)} all-gather(f32[16,3,144]{0,1,2:T(4,128)S(1)} %copy.72), channel_id=1, replica_groups=mesh['dp'=4,'tensor'=8] {'tensor'}, dimensions={2}, use_global_device_ids=true | all-gather | bytes 248832 | tf_op jit(solution)/shard_map/all_gather | solution.py:70
  86.1 0.9 slice_add_fusion
  87.2 0.2 copy.74
  87.4 18.4 %all-gather.3.cloned.1.call-done = bf16[8,256,1152]{1,2,0:T(8,128)(2,1)} async-done(((bf16[8,256,144]{1,2,0:T(8,128)(2,1)}), bf16[8,256,1152]{1,2,0:T(8,128)(2,1)}) %all-gather.3.cloned.1.call-update) | async-done | bytes 4718608 | tf_op jit(solution)/shard_map/all_gather | solution.py:125
  105.8 10.8 %fusion.31 = bf16[16,256,432]{1,2,0:T(8,128)(2,1)S(1)} fusion(bf16[8,256,1152]{1,2,0:T(8,128)(2,1)} %all-gather.3.cloned.1.call-done, f32[16,1152]{1,0:T(8,128)S(1)} %copy.74, f32[16,1152]{1,0:T(8,128)S(1)} %copy.73, bf16[1152,432]{0,1:T(8,128)(2,1)} %param.22), kind=kOutput, calls=%fused_computation.35 | convolution fusion | flops 4111663104 | bytes 9400320 | tf_op jit(solution)/shard_map/bld,df->blf/dot_general | solution.py:74
  116.6 1.7 copy-done.7
  118.4 1.3 fusion.59
  119.7 6.3 %fusion.94 = (f32[16,2,256]{2,1,0:T(2,128)S(1)}, f32[16,2,256,256]{2,3,1,0:T(8,128)S(1)}) fusion(f32[16,2,256,256]{2,3,1,0:T(8,128)S(1)} %fusion.59), kind=kOutput, calls=%fused_computation.132 | output fusion | flops 8388863 | bytes 16809984 | tf_op jit(solution)/shard_map/sub | solution.py:32
  126.0 2.3 fusion.37
  128.3 5.3 convolution_convert_fusion
  133.7 0.8 copy-done.15
  134.5 0.2 fusion.73
  134.9 0.4 fusion.95
  135.3 0.2 copy.64
  135.5 42.4 %all_gather.13 = f32[8,3,1152]{0,1,2:T(4,128)S(1)} all-gather(f32[8,3,144]{0,1,2:T(4,128)S(1)} %copy.64), channel_id=1, replica_groups=mesh['dp'=4,'tensor'=8] {'tensor'}, dimensions={2}, use_global_device_ids=true | all-gather | bytes 124416 | tf_op jit(solution)/shard_map/all_gather | solution.py:70
  177.9 0.9 slice_add_fusion.1
  179.0 0.2 copy.66
  179.3 5.9 %fusion.36 = bf16[8,256,432]{1,2,0:T(8,128)(2,1)S(1)} fusion(bf16[8,256,1152]{1,2,0:T(8,128)(2,1)} %all-gather.3.cloned.1.call-done, f32[8,1152]{1,0:T(8,128)S(1)} %copy.66, f32[8,1152]{1,0:T(8,128)S(1)} %copy.65, bf16[1152,432]{0,1:T(8,128)(2,1)S(1)} %copy-done.13), kind=kOutput, calls=%fused_computation.50 | convolution fusion | flops 2048753664 | bytes 7557120 | tf_op jit(solution)/shard_map/bld,df->blf/dot_general | solution.py:74
  185.2 0.8 fusion.65
  185.9 3.2 fusion.93
  189.2 0.5 convolution_convert_fusion.6
  189.7 1.5 copy-done.3
  191.2 3.6 convolution_convert_fusion.2
  195.1 54.8 %reduce-scatter.13.cloned.1.call-done = bf16[16,256,144]{1,2,0:T(8,128)(2,1)} async-done(((bf16[16,256,1152]{1,2,0:T(8,128)(2,1)}), bf16[16,256,144]{1,2,0:T(8,128)(2,1)}) %reduce-scatter.13.cloned.1.call-update) | async-done | bytes 1179664 | tf_op jit(solution)/shard_map/reduce_scatter | solution.py:79
  249.9 3.1 fusion.57
  253.0 54.6 %reduce-scatter.11.cloned.1.call-done = bf16[8,256,144]{1,2,0:T(8,128)(2,1)} async-done(((bf16[8,256,1152]{1,2,0:T(8,128)(2,1)}), bf16[8,256,144]{1,2,0:T(8,128)(2,1)}) %reduce-scatter.11.cloned.1.call-update) | async-done | bytes 589840 | tf_op jit(solution)/shard_map/reduce_scatter | solution.py:79
  307.6 2.7 fusion.51
  310.3 1.0 multiply_convert_fusion.2
  311.3 0.3 reduce-scatter.17.cloned.1.call-start
  311.6 49.6 %all-gather.5.cloned.1.call-done = bf16[8,256,1152]{1,2,0:T(8,128)(2,1)} async-done(((bf16[8,256,144]{1,2,0:T(8,128)(2,1)}), bf16[8,256,1152]{1,2,0:T(8,128)(2,1)}) %all-gather.5.cloned.1.call-update) | async-done | bytes 4718608 | tf_op jit(solution)/shard_map/all_gather | solution.py:142
  361.2 3.4 convolution_convert_fusion.4
  364.8 0.8 fusion.44
  365.6 3.8 fusion.66
  369.4 7.7 %fusion.48 = bf16[8,256,2,1,72]{1,4,2,0,3:T(8,128)(2,1)S(1)} fusion(f32[8,2,256,256]{2,3,1,0:T(8,128)} %fusion.66, bf16[8,256,2,3,72]{1,4,3,2,0:T(8,128)(2,1)} %bitcast.136, f32[8,2,256,256]{2,3,1,0:T(8,128)} %copy-done.3, f32[8,2,256]{2,1,0:T(2,128)S(1)} %get-tuple-element.17), kind=kOutput, calls=%fused_computation.63 | convolution fusion | flops 158634240 | bytes 17989632 | tf_op jit(solution)/shard_map/bhlm,bmhe->blhe/dot_general | solution.py:52
  377.1 7.6 %fusion.45 = bf16[8,256,2,1,72]{1,4,2,0,3:T(8,128)(2,1)S(1)} fusion(f32[8,2,256,256]{2,3,1,0:T(8,128)} %fusion.66, bf16[8,256,2,3,72]{1,4,3,2,0:T(8,128)(2,1)} %bitcast.137, f32[8,2,256,256]{2,3,1,0:T(8,128)} %copy-done.3, f32[8,2,256]{2,1,0:T(2,128)S(1)} %get-tuple-element.17), kind=kOutput, calls=%fused_computation.62 | convolution fusion | flops 158634240 | bytes 17989632 | tf_op jit(solution)/shard_map/bhlm,blhe->bmhe/dot_general | solution.py:55
  384.8 0.2 pad_maximum_fusion
  385.1 1.2 copy-done.5
  386.3 4.4 convolution_convert_fusion.1
  390.8 4.0 fusion.32
  394.7 1.1 copy.91
  395.9 6.4 %fusion.23 = bf16[1152,432]{1,0:T(8,128)(2,1)} fusion(bf16[8,256,432]{1,2,0:T(8,128)(2,1)} %bitcast.132, bf16[8,256,1152]{1,2,0:T(8,128)(2,1)} %all-gather.3.cloned.1.call-done, f32[8,1152]{1,0:T(8,128)S(1)} %copy.66, f32[8,1152]{1,0:T(8,128)S(1)} %copy.65), kind=kOutput, calls=%fused_computation.29 | convolution fusion | flops 2048366592 | bytes 7557120 | tf_op jit(solution)/shard_map/bld,blf->df/dot_general | solution.py:150
  402.3 0.3 reduce-scatter.21.cloned.1.call-start
  402.6 41.9 %reduce-scatter.17.cloned.1.call-done = bf16[8,256,144]{1,2,0:T(8,128)(2,1)} async-done(((bf16[8,256,1152]{1,2,0:T(8,128)(2,1)}), bf16[8,256,144]{1,2,0:T(8,128)(2,1)}) %reduce-scatter.17.cloned.1.call-update) | async-done | bytes 589840 | tf_op jit(solution)/shard_map/reduce_scatter | solution.py:156
  444.5 1.7 convert_reduce_fusion.1
  446.2 1.0 fusion.24
  447.2 3.2 copy.93
  450.5 5.6 %reshape.56 = bf16[1152,432]{1,0:T(8,128)(2,1)} reshape(bf16[1152,3,144]{2,1,0:T(4,128)(2,1)} %bitcast.120) | data formatting | bytes 1990656
  456.0 15.7 %reduce-scatter.19.cloned.1.call-done = bf16[288,144]{1,0:T(8,128)(2,1)} async-done(((bf16[1152,144]{1,0:T(8,128)(2,1)}), bf16[288,144]{1,0:T(8,128)(2,1)}) %reduce-scatter.19.cloned.1.call-update) | async-done | bytes 82960
  471.7 1.0 copy.92
  472.7 0.7 convert_element_type.149
  473.5 29.9 %reduce-scatter.15.cloned.1.call-done = bf16[288,432]{1,0:T(8,128)(2,1)} async-done(((bf16[1152,432]{1,0:T(8,128)(2,1)}), bf16[288,432]{1,0:T(8,128)(2,1)}) %reduce-scatter.15.cloned.1.call-update) | async-done | bytes 248848 | tf_op jit(solution)/shard_map/reduce_scatter | solution.py:169
  503.4 1.8 convert_element_type.147
  505.2 29.8 %reduce-scatter.21.cloned.1.call-done = bf16[288,432]{1,0:T(8,128)(2,1)} async-done(((bf16[1152,432]{1,0:T(8,128)(2,1)}), bf16[288,432]{1,0:T(8,128)(2,1)}) %reduce-scatter.21.cloned.1.call-update) | async-done | bytes 248848
  535.0 1.8 reshape.57
  536.8 0.4 copy.94
  537.2 0.9 convert_element_type.155
  (55 shorter events, 1.5 us)
Async XLA Ops:
  7.2 34.6 %copy-start = (bf16[1000,1152]{1,0:T(8,128)(2,1)S(1)}, bf16[1000,1152]{1,0:T(8,128)(2,1)}, u32[]{:S(2)}) copy-start(bf16[1000,1152]{1,0:T(8,128)(2,1)} %param.19) | copy-start | bytes 6912004
  7.2 35.7 %copy-start.12 = (s32[8]{0:T(128)S(1)}, s32[8]{0:T(128)}, u32[]{:S(2)}) copy-start(s32[8]{0:T(128)} %param.15) | copy-start | bytes 100
  7.2 37.9 %copy-start.9 = (bf16[3,1152,144]{1,2,0:T(8,128)(2,1)S(1)}, bf16[3,1152,144]{1,2,0:T(8,128)(2,1)}, u32[]{:S(2)}) copy-start(bf16[3,1152,144]{1,2,0:T(8,128)(2,1)} %param.24) | copy-start | bytes 2985988
  7.2 98.6 %all-gather.3.cloned.1.call-start = ((), (), s32[]{:S(2)}) async-start(), calls=%async_computation.6 | async-start | bytes 5308416 | tf_op jit(solution)/shard_map/all_gather | solution.py:125
  41.0 208.9 %reduce-scatter.13.cloned.1.call-start = ((), (), s32[]{:S(2)}) async-start(), calls=%async_computation.8 | async-start | bytes 10616832 | tf_op jit(solution)/shard_map/reduce_scatter | solution.py:79
  116.6 1.8 copy-start.7
  126.0 2.3 copy-start.11
  133.6 0.9 copy-start.15
  133.6 0.9 copy-start.16
  133.6 1.3 copy-start.10
  133.7 45.6 %copy-start.13 = (bf16[1152,432]{0,1:T(8,128)(2,1)S(1)}, bf16[1152,432]{0,1:T(8,128)(2,1)}, u32[]{:S(2)}) copy-start(bf16[1152,432]{0,1:T(8,128)(2,1)} %param.25) | copy-start | bytes 2985988
  133.7 173.9 %reduce-scatter.11.cloned.1.call-start = ((), (), s32[]{:S(2)}) async-start(), calls=%async_computation.7 | async-start | bytes 5308416 | tf_op jit(solution)/shard_map/reduce_scatter | solution.py:79
  185.2 4.0 copy-start.6
  189.2 2.0 copy-start.3
  189.2 2.0 copy-start.8
  191.2 3.7 copy-start.17
  194.8 112.8 %copy-start.2 = (bf16[8,256,144]{1,2,0:T(8,128)(2,1)S(1)}, bf16[8,256,144]{1,2,0:T(8,128)(2,1)}, u32[]{:S(2)}) copy-start(bf16[8,256,144]{1,2,0:T(8,128)(2,1)} %param.14) | copy-start | bytes 1769476
  194.9 166.3 %all-gather.5.cloned.1.call-start = ((), (), s32[]{:S(2)}) async-start(), calls=%async_computation.9 | async-start | bytes 5308416 | tf_op jit(solution)/shard_map/all_gather | solution.py:142
  311.3 133.2 %reduce-scatter.17.cloned.1.call-start = ((), (), s32[]{:S(2)}) async-start(), calls=%async_computation.11 | async-start | bytes 5308416 | tf_op jit(solution)/shard_map/reduce_scatter | solution.py:156
  361.2 3.6 copy-start.4
  384.7 1.5 copy-start.14
  385.1 1.2 copy-start.5
  390.7 81.0 %reduce-scatter.19.cloned.1.call-start = ((), (), s32[]{:S(2)}) async-start(), calls=%async_computation.12 | async-start | bytes 737280
  395.8 107.5 %reduce-scatter.15.cloned.1.call-start = ((), (), s32[]{:S(2)}) async-start(), calls=%async_computation.10 | async-start | bytes 1474560 | tf_op jit(solution)/shard_map/reduce_scatter | solution.py:169
  402.3 132.7 %reduce-scatter.21.cloned.1.call-start = ((), (), s32[]{:S(2)}) async-start(), calls=%async_computation.13 | async-start | bytes 1474560
  450.5 87.6 %copy-start.1 = (bf16[1000,1152]{1,0:T(8,128)(2,1)S(1)}, bf16[1000,1152]{1,0:T(8,128)(2,1)}, u32[]{:S(2)}) copy-start(bf16[1000,1152]{1,0:T(8,128)(2,1)} %param.19) | copy-start | bytes 6912004
Sparse Core Ops, SparseCore 0:
  41.1 64.6 all-gather.2
  133.8 116.0 reduce-scatter.12
  252.2 55.3 reduce-scatter.10
  311.5 49.6 all-gather.4
  390.9 53.6 reduce-scatter.16
  447.8 23.8 reduce-scatter.18
  474.6 28.6 reduce-scatter.14
  506.3 28.6 reduce-scatter.20
where the time goes:
time: 546 us; the launch traced here: 545 us
  waiting for transfers between devices  295 us (54%)
  blocking collectives  113 us (21%)
  matrix products  73.9 us (14%)
  other arithmetic  27.9 us (5%)
  local copies, waits for them, and re-layouts  19.9 us (4%)
  between operations  14.5 us (3%)
    reduce_scatter x2, waiting for transfers between devices, forward(): lax.psum_scatter(partial_value.astype(jnp.bfloat16), 'tensor', scatter_di...  109 us
    all_gather x2, blocking collectives, forward(): wide_mod = lax.all_gather(modulation, 'tensor', axis=2, tiled=True)  82.8 us
    all_gather x1, waiting for transfers between devices, local(): gathered = lax.all_gather(grad_proj, 'tensor', axis=2, tiled=True)  49.6 us
    unnamed x10, waiting for transfers between devices  45.6 us
    reduce_scatter x1, waiting for transfers between devices, local(): lax.psum_scatter(input_terms.astype(jnp.bfloat16), 'tensor', scatter_dime...  41.9 us
    psum x1, blocking collectives, local(): lax.psum((jnp.sum(signal, axis=2), jnp.sum(signal * signal, axis=2)), 'te...  30.3 us
    reduce_scatter x1, waiting for transfers between devices, local(): lax.psum_scatter(grad_qkv_local.astype(jnp.bfloat16), 'dp', scatter_dimen...  29.9 us
    unnamed x42, local copies, waits for them, and re-layouts  18.7 us
  transfers between devices with their start and end apart: 8, of which 8 were waited for; matrix products, arithmetic and copies ran while one was open for 10% of the time, Pallas kernels for 0%

commit v1 on v0

v1 whole, which is shorter than its diff:
```python
import math

import jax
import jax.numpy as jnp
from jax import lax
from jax.experimental import pallas as pl
from jax.experimental.pallas import tpu as pltpu
from jax.sharding import PartitionSpec as P

HD = 72


norm_eps = 1e-06


def lookup_rows(indices, table_rows):
    one_hot = (
        indices[:, None] == jnp.arange(table_rows.shape[0], dtype=jnp.int32)[None, :]
    ).astype(table_rows.dtype)
    return jnp.dot(one_hot, table_rows, preferred_element_type=jnp.float32)


def attend(qkv_sums, heads_here):
    batch_rows, seq_len = (qkv_sums.shape[0], qkv_sums.shape[1])
    heads_qkv = qkv_sums.astype(jnp.bfloat16).reshape(batch_rows, seq_len, heads_here, 3, HD)
    queries, key_rows, values = (
        heads_qkv[:, :, :, 0],
        heads_qkv[:, :, :, 1],
        heads_qkv[:, :, :, 2],
    )
    scores = jnp.einsum(
        "blhe,bmhe->bhlm", queries, key_rows, preferred_element_type=jnp.float32
    ) * (1.0 / math.sqrt(HD))
    exponent = jnp.exp(scores - jnp.max(scores, axis=-1, keepdims=True))
    attn_prob = exponent / jnp.sum(exponent, axis=-1, keepdims=True)
    prob_low = attn_prob.astype(jnp.bfloat16)
    attn_mixed = jnp.einsum("bhlm,bmhe->blhe", prob_low, values, preferred_element_type=jnp.float32)
    attn_mixed = attn_mixed.astype(jnp.bfloat16).reshape(batch_rows, seq_len, heads_here * HD)
    return (heads_qkv, attn_prob, prob_low, attn_mixed)


def attend_grad(heads_qkv, attn_prob, prob_low, grad_low):
    batch_rows, seq_len = (heads_qkv.shape[0], heads_qkv.shape[1])
    queries, key_rows, values = (
        heads_qkv[:, :, :, 0],
        heads_qkv[:, :, :, 1],
        heads_qkv[:, :, :, 2],
    )
    grad_probs = jnp.einsum("blhe,bmhe->bhlm", grad_low, values, preferred_element_type=jnp.float32)
    row_delta = jnp.sum(attn_prob * grad_probs, axis=-1, keepdims=True)
    grad_scores = (attn_prob * (grad_probs - row_delta) * (1.0 / math.sqrt(HD))).astype(
        jnp.bfloat16
    )
    grad_query = jnp.einsum(
        "bhlm,bmhe->blhe", grad_scores, key_rows, preferred_element_type=jnp.float32
    )
    grad_keys = jnp.einsum(
        "bhlm,blhe->bmhe", grad_scores, queries, preferred_element_type=jnp.float32
    )
    grad_values = jnp.einsum(
        "bhlm,blhe->bmhe", prob_low, grad_low, preferred_element_type=jnp.float32
    )
    grad_qkv_act = jnp.stack([grad_query, grad_keys, grad_values], axis=3).astype(jnp.bfloat16)
    return grad_qkv_act.reshape(batch_rows, seq_len, -1)


def modulate(normed, scale, shift):
    return (normed.astype(jnp.float32) * (1.0 + scale[:, None]) + shift[:, None]).astype(
        jnp.bfloat16
    )


def project_qkv(full_rows, qkv_weight):
    return jnp.einsum("bld,df->blf", full_rows, qkv_weight, preferred_element_type=jnp.float32)


def weight_grad_kernel(act_ref, grad_ref, scale_ref, shift_ref, weight_ref, sum_ref, mod_ref):
    @pl.when(pl.program_id(0) == 0)
    def _():
        sum_ref[...] = jnp.zeros_like(sum_ref)

    grads = grad_ref[0]
    over_tokens = lax.dot_general(
        grads,
        jnp.ones((grads.shape[0], 128), jnp.bfloat16),
        (((0,), (0,)), ((), ())),
        preferred_element_type=jnp.float32,
    )[:, :1]
    width = act_ref.shape[2]
    step = 384 if width % 384 == 0 else 128
    for start in range(0, width, step):
        cols = pl.ds(start, step)
        product = lax.dot_general(
            grads, act_ref[0, :, cols], (((0,), (0,)), ((), ())), preferred_element_type=jnp.float32
        )
        weight = weight_ref[:, cols].astype(jnp.float32)
        mod_ref[0, 0:1, cols] = jnp.sum(weight * over_tokens, axis=0, keepdims=True)
        mod_ref[0, 1:2, cols] = jnp.sum(weight * product, axis=0, keepdims=True)
        sum_ref[:, cols] += product * (1.0 + scale_ref[0, :, cols]) + over_tokens * shift_ref[
            0, :, cols
        ]


def weight_grad(normed, grad_qkv_act, scale, shift, weight_t):
    samples, seq_len, width = normed.shape
    columns = grad_qkv_act.shape[2]
    return pl.pallas_call(
        weight_grad_kernel,
        grid=(samples,),
        in_specs=[
            pl.BlockSpec((1, seq_len, width), lambda b: (b, 0, 0)),
            pl.BlockSpec((1, seq_len, columns), lambda b: (b, 0, 0)),
            pl.BlockSpec((1, 1, width), lambda b: (b, 0, 0)),
            pl.BlockSpec((1, 1, width), lambda b: (b, 0, 0)),
            pl.BlockSpec((columns, width), lambda b: (0, 0)),
        ],
        out_specs=[
            pl.BlockSpec((columns, width), lambda b: (0, 0)),
            pl.BlockSpec((1, 2, width), lambda b: (b, 0, 0)),
        ],
        out_shape=[
            jax.ShapeDtypeStruct((columns, width), jnp.float32),
            jax.ShapeDtypeStruct((samples, 2, width), jnp.float32),
        ],
        compiler_params=pltpu.CompilerParams(
            dimension_semantics=("arbitrary",), vmem_limit_bytes=32 * 1024 * 1024
        ),
        cost_estimate=pl.CostEstimate(
            flops=2 * samples * seq_len * width * columns,
            bytes_accessed=samples * seq_len * (width + columns) * 2 + width * columns * 6,
            transcendentals=0,
        ),
    )(normed, grad_qkv_act, scale[:, None], shift[:, None], weight_t)


def local(
    noisy,
    labels,
    tsteps,
    guide_index,
    class_table,
    time_table,
    guide_table,
    guide_weights,
    teacher_qkv,
    teacher_out,
    teacher_ada,
    student_qkv,
    student_out,
    student_ada,
):
    samples, seq_len, width_part = noisy.shape
    ways = lax.axis_size("tensor")
    groups = lax.axis_size("dp")
    me = lax.axis_index("tensor")
    model_width = width_part * ways
    batch_size = samples * groups
    wide_noisy = lax.all_gather(noisy, "tensor", axis=2, tiled=True)

    null_class = class_table.shape[0] - 1
    time_embed = lookup_rows(tsteps, time_table)
    cond_embed = lookup_rows(labels, class_table) + time_embed
    null_embed = class_table[null_class].astype(jnp.float32)[None, :] + time_embed
    guide_hot = guide_index[:, None] == jnp.arange(guide_table.shape[0], dtype=jnp.int32)[None, :]
    student_embed = cond_embed + jnp.dot(
        guide_hot.astype(jnp.bfloat16), guide_table, preferred_element_type=jnp.float32
    )
    strength = jnp.sum(jnp.where(guide_hot, guide_weights[None, :], 0.0), axis=1)
    cond_act = jax.nn.silu(cond_embed).astype(jnp.bfloat16)
    null_act = jax.nn.silu(null_embed).astype(jnp.bfloat16)
    student_act = jax.nn.silu(student_embed).astype(jnp.bfloat16)
    teacher_act = jnp.concatenate([cond_act, null_act], axis=0)
    mod_teacher = jnp.einsum(
        "bd,kde->kbe", teacher_act, teacher_ada, preferred_element_type=jnp.float32
    )
    mod_student = jnp.einsum(
        "bd,kde->kbe", student_act, student_ada, preferred_element_type=jnp.float32
    )
    mods = jnp.concatenate([mod_student, mod_teacher], axis=1).reshape(-1, width_part)
    wide_mods = gather_mods(mods).reshape(3, 3, samples, model_width)
    shift, scale, gate = wide_mods[0], wide_mods[1], wide_mods[2]

    teacher_out_full = lax.all_gather(teacher_out, "tensor", axis=0, tiled=True)
    student_out_full = lax.all_gather(student_out, "tensor", axis=0, tiled=True)

    signal = wide_noisy.astype(jnp.float32)
    row_mean = jnp.sum(signal, axis=2, keepdims=True) / model_width
    row_var = jnp.sum(signal * signal, axis=2, keepdims=True) / model_width - row_mean * row_mean
    normed = ((signal - row_mean) * lax.rsqrt(row_var + norm_eps)).astype(jnp.bfloat16)
    normed = lax.optimization_barrier(normed)

    heads_here = student_out.shape[0] // HD
    teacher_rows = jnp.concatenate(
        [modulate(normed, scale[1], shift[1]), modulate(normed, scale[2], shift[2])], axis=0
    )
    unused_qkv, unused_prob, unused_low, teacher_mixed = attend(
        project_qkv(teacher_rows, teacher_qkv), heads_here
    )
    student_rows = modulate(normed, scale[0], shift[0])
    heads_qkv, attn_prob, prob_low, student_mixed = attend(
        project_qkv(student_rows, student_qkv), heads_here
    )
    head_cols = heads_here * HD
    mixed = jnp.concatenate([student_mixed, teacher_mixed], axis=0).reshape(
        3, samples * seq_len, head_cols
    )
    mixed_rows = lax.all_to_all(mixed, "tensor", split_axis=1, concat_axis=2, tiled=True)

    row_count = samples * seq_len // ways
    run = min(row_count, seq_len)
    images = row_count // run
    first = me * row_count // seq_len
    own_gate = lax.dynamic_slice_in_dim(gate, first, images, axis=1)
    own_strength = lax.dynamic_slice_in_dim(strength, first, images, axis=0)[:, None]
    student_proj = jnp.dot(mixed_rows[0], student_out_full, preferred_element_type=jnp.float32)
    teacher_proj = jnp.einsum(
        "kre,ed->krd", mixed_rows[1:], teacher_out_full, preferred_element_type=jnp.float32
    ).reshape(2, images, run, model_width)
    student_proj = student_proj.reshape(images, run, model_width)
    scale_norm = 1.0 / math.sqrt(batch_size * seq_len)
    cotangent = scale_norm * (
        own_gate[0][:, None] * student_proj
        - ((1.0 + own_strength) * own_gate[1])[:, None] * teacher_proj[0]
        + (own_strength * own_gate[2])[:, None] * teacher_proj[1]
    )
    own_grad_gate = jnp.sum(cotangent * student_proj, axis=1)
    grad_proj = (
        (cotangent * own_gate[0][:, None]).astype(jnp.bfloat16).reshape(row_count, model_width)
    )
    grad_mixed_rows = lax.dot_general(
        grad_proj, student_out_full, (((1,), (1,)), ((), ())), preferred_element_type=jnp.float32
    ).astype(jnp.bfloat16)
    grad_low = lax.all_to_all(grad_mixed_rows, "tensor", split_axis=1, concat_axis=0, tiled=True)
    grad_low = grad_low.reshape(samples, seq_len, heads_here, HD)
    grad_out_part = lax.dot_general(
        mixed_rows[0], grad_proj, (((0,), (0,)), ((), ())), preferred_element_type=jnp.float32
    ).astype(jnp.bfloat16)
    grad_out = lax.psum_scatter(grad_out_part, "tensor", scatter_dimension=0, tiled=True)
    grad_out = lax.psum_scatter(grad_out, "dp", scatter_dimension=1, tiled=True).astype(jnp.float32)

    grad_qkv_act = attend_grad(heads_qkv, attn_prob, prob_low, grad_low)
    grad_qkv_t, grad_mod = weight_grad(normed, grad_qkv_act, scale[0], shift[0], student_qkv.T)
    grad_qkv = lax.psum_scatter(
        grad_qkv_t.T.astype(jnp.bfloat16), "dp", scatter_dimension=0, tiled=True
    ).astype(jnp.float32)

    grad_gate = lax.dynamic_update_slice_in_dim(
        jnp.zeros((samples, model_width), jnp.float32), own_grad_gate, first, axis=0
    )
    grad_mod = jnp.concatenate([grad_mod, grad_gate[:, None]], axis=1)
    act_all = lax.all_gather(student_act, "dp", axis=0, tiled=True)
    wide_grad = lax.psum_scatter(grad_mod, "tensor", scatter_dimension=2, tiled=True)
    wide_grad = lax.all_gather(wide_grad, "dp", axis=0, tiled=True)
    act_cols = model_width // groups
    own_act = lax.dynamic_slice_in_dim(act_all, lax.axis_index("dp") * act_cols, act_cols, axis=1)
    grad_ada = jnp.einsum(
        "bd,bke->kde",
        own_act.astype(jnp.float32),
        wide_grad,
        precision=lax.Precision.HIGHEST,
    )
    return (grad_qkv, grad_out, grad_ada)


def gather_mods(mods):
    gathered = lax.all_gather(mods, "tensor", axis=0)
    return gathered.transpose(1, 0, 2)


def solution(mesh):
    return jax.shard_map(
        local,
        mesh=mesh,
        in_specs=(
            P("dp", None, "tensor"),
            P("dp"),
            P("dp"),
            P("dp"),
            P(),
            P(),
            P(),
            P(),
            P(None, "tensor"),
            P("tensor", None),
            P(None, None, "tensor"),
            P(None, "tensor"),
            P("tensor", None),
            P(None, None, "tensor"),
        ),
        out_specs=(P("dp", "tensor"), P("tensor", "dp"), P(None, "dp", "tensor")),
        check_vma=False,
    )
```

time: 546 us -> 380 us (0.70)
  waiting for transfers between devices: 295 us -> 157 us
  blocking collectives: 113 us -> 37.1 us
  local copies, waits for them, and re-layouts: 19.9 us -> 72.2 us
  matrix products: 73.9 us -> 61 us
  Pallas kernels: 0 us -> 7.87 us
  other arithmetic: 27.9 us -> 20.4 us
  starting transfers between devices: 0.81 us -> 7.41 us
    reduce_scatter x4 -> x1, waiting for transfers between devices: 181 us -> 0.02 us  [local(): lax.psum_scatter(grad_out_part, 'tensor', scatter_dimension=0, tiled=True)]
    all_to_all x0 -> x2, waiting for transfers between devices: none -> 64.8 us  [the longest x1 38.6 us: local(): lax.all_to_all(mixed, 'tensor', split_axis=1, concat_axis=2, tiled=True)]
    all_gather x2 -> x3, blocking collectives: 82.8 us -> 37.1 us  [the longest x1 20.1 us: gather_mods(): gathered = lax.all_gather(mods, 'tensor', axis=0)]
    all_gather x2 -> x3, waiting for transfers between devices: 67.9 us -> 30.3 us  [the longest x1 30.3 us: local(): wide_noisy = lax.all_gather(noisy, 'tensor', axis=2, tiled=True)]
    psum x1 -> x0, blocking collectives: 30.3 us -> none  [local(): lax.psum((jnp.sum(signal, axis=2), jnp.sum(signal * signal, axis=2)), 'te...]
    dot_general x11 -> x9, matrix products: 45.7 us -> 25.1 us  [the longest x2 9.08 us: project_qkv(): jnp.einsum('bld,df->blf', full_rows, qkv_weight, preferred_element_type=j...]
    unnamed x42 -> x49, local copies, waits for them, and re-layouts: 18.7 us -> 38.2 us
    unnamed x10, waiting for transfers between devices: 45.6 us -> 61.7 us
  transfers between devices with their start and end apart: 8 -> 9, of which waited for: 8 -> 6; matrix products, arithmetic and copies ran while one was open for 10% -> 37% of each run, Pallas kernels for 0% -> 2%
where the time goes in v1:
time: 380 us; the launch traced here: 378 us
  waiting for transfers between devices  157 us (41%)
  local copies, waits for them, and re-layouts  72.2 us (19%)
  matrix products  61 us (16%)
  blocking collectives  37.1 us (10%)
  other arithmetic  20.4 us (5%)
  between operations  15.4 us (4%)
  Pallas kernels  7.87 us (2%)
  starting transfers between devices  7.41 us (2%)
    unnamed x10, waiting for transfers between devices  61.7 us
    all_to_all x1, waiting for transfers between devices, local(): lax.all_to_all(mixed, 'tensor', split_axis=1, concat_axis=2, tiled=True)  38.6 us
    unnamed x49, local copies, waits for them, and re-layouts  38.2 us
    all_gather x1, waiting for transfers between devices, local(): wide_noisy = lax.all_gather(noisy, 'tensor', axis=2, tiled=True)  30.3 us
    all_to_all x1, waiting for transfers between devices, local(): lax.all_to_all(grad_mixed_rows, 'tensor', split_axis=1, concat_axis=0, ti...  26.2 us
    all_gather x1, blocking collectives, gather_mods(): gathered = lax.all_gather(mods, 'tensor', axis=0)  20.1 us
    reshape x2, local copies, waits for them, and re-layouts, local(): jnp.concatenate([student_mixed, teacher_mixed], axis=0)  12.7 us
    dot_general x2, matrix products, project_qkv(): jnp.einsum('bld,df->blf', full_rows, qkv_weight, preferred_element_type=j...  9.08 us
  transfers between devices with their start and end apart: 9, of which 6 were waited for; matrix products, arithmetic and copies ran while one was open for 37% of the time, Pallas kernels for 2%

profile of v1, /device:TPU:0, one launch (start us, length us, event | category | flops | bytes accessed | tf_op | source)
XLA Modules:
  0.0 378.3 jit_solution(2173368192680059759)
XLA Ops:
  7.3 2.2 copy.153
  9.5 0.7 all-gather.8.cloned.1.call-update
  10.3 0.7 all-gather.6.cloned.1.call-update
  11.0 0.8 convert_reduce_fusion.1
  11.8 1.1 multiply_convert_fusion.4
  13.0 2.1 multiply_convert_fusion.5
  15.3 0.4 convolution_bitcast_fusion.2
  16.2 20.1 %all_gather.19 = f32[8,72,144]{2,1,0:T(8,128)S(1)} all-gather(f32[1,72,144]{2,1,0:T(8,128)S(1)} %bitcast.156), channel_id=1, replica_groups=mesh['dp'=4,'tensor'=8] {'tensor'}, dimensions={0}, use_global_device_ids=true | all-gather | bytes 373248 | tf_op jit(solution)/shard_map/all_gather | solution.py:266
  37.1 30.3 %all-gather.4.cloned.1.call-done = bf16[8,256,1152]{1,0,2:T(8,128)(2,1)} async-done(((bf16[8,256,144]{1,0,2:T(8,128)(2,1)}), bf16[8,256,1152]{1,0,2:T(8,128)(2,1)}) %all-gather.4.cloned.1.call-update) | async-done | bytes 4718608 | tf_op jit(solution)/shard_map/all_gather | solution.py:158
  67.4 7.1 %copy.154 = bf16[8,256,1152]{2,1,0:T(8,128)(2,1)} copy(bf16[8,256,1152]{1,0,2:T(8,128)(2,1)} %all-gather.4.cloned.1.call-done) | data formatting | bytes 9437184 | tf_op jit(solution)/shard_map/all_gather | solution.py:158
  74.5 4.1 %convert_reduce_fusion = (f32[8,256]{1,0:T(8,128)S(1)}, f32[8,256]{1,0:T(8,128)S(1)}) fusion(bf16[8,256,1152]{2,1,0:T(8,128)(2,1)} %copy.154), kind=kLoop, calls=%fused_computation.8 | loop fusion | flops 9433088 | bytes 4734976 | tf_op jit(solution)/shard_map/reduce_sum | solution.py:187
  78.7 1.3 fusion.4.act_ref
  80.0 2.6 fusion.9
  82.6 6.5 %fusion.39 = bf16[16,256,432]{1,2,0:T(8,128)(2,1)} fusion(bf16[8,256,1152]{2,1,0:T(8,128)(2,1)S(1)} %get-tuple-element.33, bf16[8,256,1152]{2,1,0:T(8,128)(2,1)S(1)} %get-tuple-element.32, bf16[1152,432]{0,1:T(8,128)(2,1)S(1)} %copy-done.15), kind=kOutput, calls=%fused_computation.43 | convolution fusion | flops 4083351552 | bytes 13971456 | tf_op jit(solution)/shard_map/bld,df->blf/dot_general | solution.py:74
  89.1 2.9 fusion.66
  92.0 4.5 %fusion.95 = (f32[16,2,256]{2,1,0:T(2,128)S(1)}, f32[16,2,256,256]{2,3,1,0:T(8,128)}) fusion(f32[16,2,256,256]{2,3,1,0:T(8,128)S(1)} %fusion.66), kind=kOutput, calls=%fused_computation.128 | output fusion | flops 8388863 | bytes 16809984 | tf_op jit(solution)/shard_map/sub | solution.py:34
  96.6 4.8 %fusion.48 = bf16[16,2,72,256]{3,2,1,0:T(8,128)(2,1)S(1)} fusion(f32[16,2,256,256]{2,3,1,0:T(8,128)} %get-tuple-element.48, f32[16,2,256]{2,1,0:T(2,128)S(1)} %get-tuple-element.47, bf16[16,256,2,3,72]{1,4,3,2,0:T(8,128)(2,1)} %bitcast.153), kind=kOutput, calls=%fused_computation.53 | convolution fusion | flops 306774016 | bytes 10780672 | tf_op jit(solution)/shard_map/bhlm,bmhe->blhe/dot_general | solution.py:37
  101.8 2.6 fusion.45
  104.3 0.8 fusion.71
  105.1 3.2 fusion.96
  108.4 0.5 convolution_convert_fusion.3
  108.9 1.5 copy-done.7
  110.7 2.8 reshape.157
  113.5 9.9 %copy.172 = bf16[3,2048,144]{2,0,1:T(4,128)(2,1)} copy(bf16[3,2048,144]{1,0,2:T(4,128)(2,1)} %reshape.157) | data formatting | bytes 3538944 | tf_op jit(solution)/shard_map/reshape | solution.py:204
  123.4 8.6 %reshape.176 = bf16[8,2,55296]{2,1,0:T(2,128)(2,1)} reshape(bf16[2048,3,144]{2,1,0:T(4,128)(2,1)} %bitcast.133) | data formatting | bytes 3538944
  132.0 3.6 all-to-all-start
  135.7 0.9 slice.119
  137.1 0.6 dynamic_slice.10
  138.3 0.7 dynamic-slice_reduce_fusion
  139.0 38.6 %all-to-all-done = bf16[8,2,55296]{2,1,0:T(2,128)(2,1)S(1)} async-done(((bf16[8,2,55296]{2,1,0:T(2,128)(2,1)}), bf16[8,2,55296]{2,1,0:T(2,128)(2,1)S(1)}, u32[]{:S(2)}, u32[]{:S(2)}) %all-to-all-start) | async-done | bytes 1769504 | tf_op jit(solution)/shard_map/all_to_all | solution.py:207
  177.6 6.8 %reshape.177 = bf16[2048,3,144]{2,1,0:T(4,128)(2,1)} reshape(bf16[8,2,55296]{2,1,0:T(2,128)(2,1)S(1)} %all-to-all-done) | data formatting | bytes 3538944
  184.4 4.9 %copy.193 = bf16[3,8,256,144]{2,1,3,0:T(8,128)(2,1)S(1)} copy(bf16[3,8,256,144]{3,0,2,1:T(4,128)(2,1)} %bitcast.134) | data formatting | bytes 3538944 | tf_op jit(solution)/shard_map/all_to_all | solution.py:207
  189.8 5.0 %fusion.31 = f32[2,256,1152]{2,1,0:T(8,128)} fusion(bf16[2,256,1152]{1,2,0:T(8,128)(2,1)S(1)} %bitcast.138, bf16[1152,1152]{1,0:T(8,128)(2,1)} %all-gather.8.cloned.1.call-done), kind=kOutput, calls=%fused_computation.38 | convolution fusion | flops 1358954496 | bytes 6193152 | tf_op jit(solution)/shard_map/kre,ed->krd/dot_general | solution.py:216
  194.8 3.6 multiply_reduce_fusion.3
  198.5 2.4 convolution_convert_fusion
  200.9 2.8 convolution_convert_fusion.1
  203.7 1.1 copy.177
  204.8 3.5 all-to-all-start.1
  208.7 26.2 %all-to-all-done.1 = bf16[256,8,144]{0,2,1:T(8,128)(2,1)S(1)} async-done(((bf16[256,8,144]{0,2,1:T(8,128)(2,1)}), bf16[256,8,144]{0,2,1:T(8,128)(2,1)S(1)}, u32[]{:S(2)}, u32[]{:S(2)}) %all-to-all-start.1) | async-done | bytes 589856 | tf_op jit(solution)/shard_map/all_to_all | solution.py:233
  235.0 3.9 %fusion.72 = f32[8,2,256,256]{2,3,1,0:T(8,128)} fusion(bf16[8,256,2,72]{1,3,2,0:T(8,128)(2,1)S(1)} %bitcast.145, bf16[8,256,2,3,72]{1,4,3,2,0:T(8,128)(2,1)} %bitcast.149), kind=kOutput, calls=%fused_computation.85 | convolution fusion | flops 150994944 | bytes 5373952 | tf_op jit(solution)/shard_map/blhe,bmhe->bhlm/dot_general | solution.py:49
  238.8 8.3 %fusion.59 = bf16[8,256,2,1,72]{1,4,2,0,3:T(8,128)(2,1)} fusion(f32[8,2,256,256]{2,3,1,0:T(8,128)} %fusion.72, bf16[8,256,2,3,72]{1,4,3,2,0:T(8,128)(2,1)} %bitcast.150, f32[8,2,256,256]{2,3,1,0:T(8,128)} %copy-done.7, f32[8,2,256]{2,1,0:T(2,128)S(1)} %get-tuple-element.49), kind=kOutput, calls=%fused_computation.61 | convolution fusion | flops 158634240 | bytes 17989632 | tf_op jit(solution)/shard_map/bhlm,bmhe->blhe/dot_general | solution.py:54
  247.2 8.2 %fusion.56 = bf16[8,256,2,1,72]{1,4,2,0,3:T(8,128)(2,1)} fusion(f32[8,2,256,256]{2,3,1,0:T(8,128)} %fusion.72, bf16[8,256,2,3,72]{1,4,3,2,0:T(8,128)(2,1)} %bitcast.151, f32[8,2,256,256]{2,3,1,0:T(8,128)} %copy-done.7, f32[8,2,256]{2,1,0:T(2,128)S(1)} %get-tuple-element.49), kind=kOutput, calls=%fused_computation.60 | convolution fusion | flops 158634240 | bytes 17989632 | tf_op jit(solution)/shard_map/bhlm,blhe->bmhe/dot_general | solution.py:57
  255.4 3.1 fusion.55
  258.7 1.4 copy.181
  260.0 2.8 copy.184.grad_ref
  262.8 2.3 copy-done.3
  265.1 7.9 %shard_map.157 = (f32[432,1152]{1,0:T(8,128)S(1)}, f32[8,2,1152]{2,1,0:T(2,128)S(1)}) custom-call(bf16[8,256,1152]{2,1,0:T(8,128)(2,1)S(1)} %copy-done.3, bf16[8,256,432]{2,1,0:T(8,128)(2,1)S(1)} %copy.184.grad_ref, f32[8,1,1152]{2,1,0:T(1,128)S(1)} %broadcast_in_dim_squeeze.4.scale_ref, f32[8,1,1152]{2,1,0:T(1,128)S(1)} %broadcast_in_dim_squeeze.5.shift_ref, ...), custom_call_target="tpu_custom_call" | custom-call | flops 2038431744 | bytes 9474048 | tf_op jit(solution)/shard_map/pallas_call | solution.py:107
  273.0 1.4 copy-done.4
  274.5 3.0 copy.198
  277.5 4.3 %reshape.170 = f32[1152,24]{1,0:T(8,128)} reshape(f32[1152,8,3]{2,1,0:T(8,128)} %bitcast.132) | data formatting | bytes 221184
  281.8 1.8 convert_bitcast_fusion
  283.6 1.7 copy.194
  285.4 2.0 copy.196
  287.5 8.4 %all_gather.23 = bf16[32,1152]{1,0:T(8,128)(2,1)S(1)} all-gather(bf16[8,1152]{1,0:T(8,128)(2,1)S(1)} %multiply_convert_fusion.6), channel_id=1, replica_groups=mesh['dp'=4,'tensor'=8] {'dp'}, dimensions={0}, use_global_device_ids=true | all-gather | bytes 92160 | tf_op jit(solution)/shard_map/all_gather | solution.py:251
  295.8 15.9 %reduce-scatter.17.cloned.1.call-done = f32[144,24]{1,0:T(8,128)} async-done(((f32[1152,24]{1,0:T(8,128)}), f32[144,24]{1,0:T(8,128)}) %reduce-scatter.17.cloned.1.call-update) | async-done | bytes 13840
  311.8 1.1 reshape.171
  313.2 8.6 %all_gather.22 = f32[32,3,144]{2,0,1:T(8,128)S(1)} all-gather(f32[8,3,144]{2,0,1:T(8,128)S(1)} %copy.185), channel_id=1, replica_groups=mesh['dp'=4,'tensor'=8] {'dp'}, dimensions={0}, use_global_device_ids=true | all-gather | bytes 69120 | tf_op jit(solution)/shard_map/all_gather | solution.py:253
  321.8 1.4 convolution_bitcast_fusion
  323.2 18.2 %reduce-scatter.13.cloned.1.call-done = bf16[288,432]{1,0:T(8,128)(2,1)} async-done(((bf16[1152,432]{1,0:T(8,128)(2,1)}), bf16[288,432]{1,0:T(8,128)(2,1)}) %reduce-scatter.13.cloned.1.call-update) | async-done | bytes 248848
  341.3 1.2 copy.195
  342.5 1.0 copy.186
  343.5 26.2 %reduce-scatter.15.cloned.1.call-done = bf16[288,144]{1,0:T(8,128)(2,1)} async-done(((bf16[1152,144]{1,0:T(8,128)(2,1)}), bf16[288,144]{1,0:T(8,128)(2,1)}) %reduce-scatter.15.cloned.1.call-update) | async-done | bytes 82960
  369.7 1.0 copy.197
  370.7 0.7 convert_element_type.114
  (86 shorter events, 4.4 us)
Async XLA Ops:
  7.2 4.7 %copy-start = (bf16[1000,1152]{1,0:T(8,128)(2,1)S(1)}, bf16[1000,1152]{1,0:T(8,128)(2,1)}, u32[]{:S(2)}) copy-start(bf16[1000,1152]{1,0:T(8,128)(2,1)} %param.19) | copy-start | bytes 6912004
  7.2 5.8 %copy-start.14 = (s32[8]{0:T(128)S(1)}, s32[8]{0:T(128)}, u32[]{:S(2)}) copy-start(s32[8]{0:T(128)} %param.15) | copy-start | bytes 100
  7.2 7.9 %copy-start.17 = (s32[8]{0:T(128)S(1)}, s32[8]{0:T(128)}, u32[]{:S(2)}) copy-start(s32[8]{0:T(128)} %param.17) | copy-start | bytes 100
  7.2 7.9 %copy-start.16 = (bf16[32,1152]{1,0:T(8,128)(2,1)S(1)}, bf16[32,1152]{1,0:T(8,128)(2,1)}, u32[]{:S(2)}) copy-start(bf16[32,1152]{1,0:T(8,128)(2,1)} %param.20) | copy-start | bytes 221188
  7.2 8.6 %copy-start.10 = (bf16[3,1152,144]{1,2,0:T(8,128)(2,1)S(1)}, bf16[3,1152,144]{1,2,0:T(8,128)(2,1)}, u32[]{:S(2)}) copy-start(bf16[3,1152,144]{1,2,0:T(8,128)(2,1)} %param.24) | copy-start | bytes 2985988
  7.2 60.2 %all-gather.4.cloned.1.call-start = ((), (), s32[]{:S(2)}) async-start(), calls=%async_computation.6 | async-start | bytes 5308416 | tf_op jit(solution)/shard_map/all_gather | solution.py:158
  9.5 180.3 %all-gather.8.cloned.1.call-start = ((), (), s32[]{:S(2)}) async-start(), calls=%async_computation.8 | async-start | bytes 2985984 | tf_op jit(solution)/shard_map/all_gather | solution.py:183
  10.3 184.6 %all-gather.6.cloned.1.call-start = ((), (), s32[]{:S(2)}) async-start(), calls=%async_computation.7 | async-start | bytes 2985984 | tf_op jit(solution)/shard_map/all_gather | solution.py:184
  11.0 4.4 %copy-start.11 = (bf16[3,1152,144]{1,2,0:T(8,128)(2,1)S(1)}, bf16[3,1152,144]{1,2,0:T(8,128)(2,1)}, u32[]{:S(2)}) copy-start(bf16[3,1152,144]{1,2,0:T(8,128)(2,1)} %param.27) | copy-start | bytes 2985988
  36.3 38.2 %copy-start.8 = (f32[8,72,144]{2,1,0:T(8,128)}, f32[8,72,144]{2,1,0:T(8,128)S(1)}, u32[]{:S(2)}) copy-start(f32[8,72,144]{2,1,0:T(8,128)S(1)} %all_gather.19) | copy-start | bytes 995332
  74.5 4.2 %copy-start.6 = (bf16[8,256,1152]{2,1,0:T(8,128)(2,1)S(1)}, bf16[8,256,1152]{2,1,0:T(8,128)(2,1)}, u32[]{:S(2)}) copy-start(bf16[8,256,1152]{2,1,0:T(8,128)(2,1)} %copy.154) | copy-start | bytes 14155780
  80.0 21.8 %copy-start.2 = (bf16[8,256,1152]{2,1,0:T(8,128)(2,1)}, bf16[8,256,1152]{2,1,0:T(8,128)(2,1)S(1)}, u32[]{:S(2)}) copy-start(bf16[8,256,1152]{2,1,0:T(8,128)(2,1)S(1)} %fusion.4.act_ref) | copy-start | bytes 14155780
  80.0 2.6 copy-start.15
  96.6 5.2 %copy-start.5 = (bf16[1152,432]{0,1:T(8,128)(2,1)S(1)}, bf16[1152,432]{0,1:T(8,128)(2,1)}, u32[]{:S(2)}) copy-start(bf16[1152,432]{0,1:T(8,128)(2,1)} %param.25) | copy-start | bytes 2985988
  104.3 4.0 %copy-start.9 = (bf16[8,256,432]{1,2,0:T(8,128)(2,1)}, bf16[8,256,432]{1,2,0:T(8,128)(2,1)S(1)}, u32[]{:S(2)}) copy-start(bf16[8,256,432]{1,2,0:T(8,128)(2,1)S(1)} %fusion.45) | copy-start | bytes 5308420
  108.3 2.1 copy-start.7
  123.4 13.4 %copy-start.18 = (f32[32]{0:T(128)S(1)}, f32[32]{0:T(128)}, u32[]{:S(2)}) copy-start(f32[32]{0:T(128)} %param.21) | copy-start | bytes 388
  132.0 45.5 %all-to-all-start = ((bf16[8,2,55296]{2,1,0:T(2,128)(2,1)}), bf16[8,2,55296]{2,1,0:T(2,128)(2,1)S(1)}, u32[]{:S(2)}, u32[]{:S(2)}) async-start(bf16[8,2,55296]{2,1,0:T(2,128)(2,1)} %reshape.176), calls=%async_computation | async-start | bytes 3538944 | tf_op jit(solution)/shard_map/all_to_all | solution.py:207
  135.6 149.8 %reduce-scatter.11.cloned.1.call-start = ((), (), s32[]{:S(2)}) async-start(), calls=%async_computation.9 | async-start | bytes 2985984 | tf_op jit(solution)/shard_map/reduce_scatter | solution.py:238
  204.8 30.2 %all-to-all-start.1 = ((bf16[256,8,144]{0,2,1:T(8,128)(2,1)}), bf16[256,8,144]{0,2,1:T(8,128)(2,1)S(1)}, u32[]{:S(2)}, u32[]{:S(2)}) async-start(bf16[256,8,144]{0,2,1:T(8,128)(2,1)} %bitcast.29), calls=%async_computation.1 | async-start | bytes 1179648 | tf_op jit(solution)/shard_map/all_to_all | solution.py:233
  208.3 103.4 %reduce-scatter.17.cloned.1.call-start = ((), (), s32[]{:S(2)}) async-start(), calls=%async_computation.12 | async-start | bytes 663552
  255.4 3.1 copy-start.12
  255.4 3.1 copy-start.13
  262.8 2.3 copy-start.3
  273.0 1.4 copy-start.4
  281.8 59.6 %reduce-scatter.13.cloned.1.call-start = ((), (), s32[]{:S(2)}) async-start(), calls=%async_computation.10 | async-start | bytes 1474560
  281.8 89.6 %copy-start.1 = (bf16[1000,1152]{1,0:T(8,128)(2,1)S(1)}, bf16[1000,1152]{1,0:T(8,128)(2,1)}, u32[]{:S(2)}) copy-start(bf16[1000,1152]{1,0:T(8,128)(2,1)} %param.19) | copy-start | bytes 6912004
  285.3 84.3 %reduce-scatter.15.cloned.1.call-start = ((), (), s32[]{:S(2)}) async-start(), calls=%async_computation.11 | async-start | bytes 737280
Sparse Core Ops, SparseCore 0:
  10.2 57.1 all-gather.3
  69.1 33.6 all-gather.7
  104.4 33.0 all-gather.5
  201.0 44.7 reduce-scatter.10
  281.9 29.8 reduce-scatter.16
  314.5 26.7 reduce-scatter.12
  344.2 25.4 reduce-scatter.14

commit v2 on v1

--- a/solution.py
+++ b/solution.py
@@ -1,3 +1,4 @@
+import functools
 import math
 
 import jax
@@ -34,8 +35,8 @@
     exponent = jnp.exp(scores - jnp.max(scores, axis=-1, keepdims=True))
     attn_prob = exponent / jnp.sum(exponent, axis=-1, keepdims=True)
     prob_low = attn_prob.astype(jnp.bfloat16)
-    attn_mixed = jnp.einsum("bhlm,bmhe->blhe", prob_low, values, preferred_element_type=jnp.float32)
-    attn_mixed = attn_mixed.astype(jnp.bfloat16).reshape(batch_rows, seq_len, heads_here * HD)
+    attn_mixed = jnp.einsum("bhlm,bmhe->bhel", prob_low, values, preferred_element_type=jnp.float32)
+    attn_mixed = attn_mixed.astype(jnp.bfloat16).reshape(batch_rows, heads_here * HD, seq_len)
     return (heads_qkv, attn_prob, prob_low, attn_mixed)
 
 
@@ -46,7 +47,7 @@
         heads_qkv[:, :, :, 1],
         heads_qkv[:, :, :, 2],
     )
-    grad_probs = jnp.einsum("blhe,bmhe->bhlm", grad_low, values, preferred_element_type=jnp.float32)
+    grad_probs = jnp.einsum("bhel,bmhe->bhlm", grad_low, values, preferred_element_type=jnp.float32)
     row_delta = jnp.sum(attn_prob * grad_probs, axis=-1, keepdims=True)
     grad_scores = (attn_prob * (grad_probs - row_delta) * (1.0 / math.sqrt(HD))).astype(
         jnp.bfloat16
@@ -58,10 +59,74 @@
         "bhlm,blhe->bmhe", grad_scores, queries, preferred_element_type=jnp.float32
     )
     grad_values = jnp.einsum(
-        "bhlm,blhe->bmhe", prob_low, grad_low, preferred_element_type=jnp.float32
+        "bhlm,bhel->bmhe", prob_low, grad_low, preferred_element_type=jnp.float32
     )
     grad_qkv_act = jnp.stack([grad_query, grad_keys, grad_values], axis=3).astype(jnp.bfloat16)
     return grad_qkv_act.reshape(batch_rows, seq_len, -1)
+
+
+def exchange_kernel(axis, slots, count, *refs):
+    sources, landings = refs[:count], refs[count : 2 * count]
+    send_sem, recv_sem, own_sem = refs[2 * count :]
+    ways = lax.axis_size(axis)
+    me = lax.axis_index(axis)
+    barrier = pltpu.get_barrier_semaphore()
+    for hop in range(1, ways):
+        peer = lax.rem(me + hop, ways)
+        pl.semaphore_signal(
+            barrier, inc=1, device_id={axis: peer}, device_id_type=pl.DeviceIdType.MESH
+        )
+    pl.semaphore_wait(barrier, ways - 1)
+    copies = []
+    for hop in range(1, ways):
+        peer = lax.rem(me + hop, ways)
+        for item in range(count):
+            take, put = slots[item]
+            copy = pltpu.make_async_remote_copy(
+                src_ref=take(sources[item], peer),
+                dst_ref=put(landings[item], me),
+                send_sem=send_sem.at[item, hop - 1],
+                recv_sem=recv_sem.at[item, hop - 1],
+                device_id={axis: peer},
+                device_id_type=pl.DeviceIdType.MESH,
+            )
+            copy.start()
+            copies.append(copy)
+    for item in range(count):
+        take, put = slots[item]
+        copy = pltpu.make_async_copy(
+            take(sources[item], me), put(landings[item], me), own_sem.at[item]
+        )
+        copy.start()
+        copies.append(copy)
+    for copy in copies:
+        copy.wait()
+
+
+def exchange(axis, collective, arrays, shapes, slots):
+    ways = lax.axis_size(axis)
+    count = len(arrays)
+    return pl.pallas_call(
+        functools.partial(exchange_kernel, axis, slots, count),
+        out_shape=[jax.ShapeDtypeStruct(s, a.dtype) for s, a in zip(shapes, arrays)],
+        in_specs=[pl.BlockSpec(memory_space=pltpu.VMEM)] * count,
+        out_specs=[pl.BlockSpec(memory_space=pltpu.VMEM)] * count,
+        scratch_shapes=[
+            pltpu.SemaphoreType.DMA((count, ways - 1)),
+            pltpu.SemaphoreType.DMA((count, ways - 1)),
+            pltpu.SemaphoreType.DMA((count,)),
+        ],
+        compiler_params=pltpu.CompilerParams(collective_id=collective, has_side_effects=True),
+        cost_estimate=pl.CostEstimate(flops=0, bytes_accessed=40000000, transcendentals=0),
+    )(*arrays)
+
+
+def block_of(ref, index):
+    return ref.at[index]
+
+
+def whole_of(ref, index):
+    return ref
 
 
 def modulate(normed, scale, shift):
@@ -74,7 +139,7 @@
     return jnp.einsum("bld,df->blf", full_rows, qkv_weight, preferred_element_type=jnp.float32)
 
 
-def weight_grad_kernel(act_ref, grad_ref, scale_ref, shift_ref, weight_ref, sum_ref, mod_ref):
+def weight_grad_kernel(act_ref, grad_ref, scale_ref, shift_ref, weight_ref, out_ref, mod_ref, sum_ref):
     @pl.when(pl.program_id(0) == 0)
     def _():
         sum_ref[...] = jnp.zeros_like(sum_ref)
@@ -100,6 +165,12 @@
             0, :, cols
         ]
 
+    @pl.when(pl.program_id(0) == pl.num_programs(0) - 1)
+    def _():
+        for start in range(0, width, step):
+            cols = pl.ds(start, step)
+            out_ref[cols, :] = sum_ref[:, cols].T.astype(out_ref.dtype)
+
 
 def weight_grad(normed, grad_qkv_act, scale, shift, weight_t):
     samples, seq_len, width = normed.shape
@@ -115,13 +186,14 @@
             pl.BlockSpec((columns, width), lambda b: (0, 0)),
         ],
         out_specs=[
-            pl.BlockSpec((columns, width), lambda b: (0, 0)),
+            pl.BlockSpec((width, columns), lambda b: (0, 0)),
             pl.BlockSpec((1, 2, width), lambda b: (b, 0, 0)),
         ],
         out_shape=[
-            jax.ShapeDtypeStruct((columns, width), jnp.float32),
+            jax.ShapeDtypeStruct((width, columns), jnp.bfloat16),
             jax.ShapeDtypeStruct((samples, 2, width), jnp.float32),
         ],
+        scratch_shapes=[pltpu.VMEM((columns, width), jnp.float32)],
         compiler_params=pltpu.CompilerParams(
             dimension_semantics=("arbitrary",), vmem_limit_bytes=32 * 1024 * 1024
         ),
@@ -201,22 +273,40 @@
         project_qkv(student_rows, student_qkv), heads_here
     )
     head_cols = heads_here * HD
-    mixed = jnp.concatenate([student_mixed, teacher_mixed], axis=0).reshape(
-        3, samples * seq_len, head_cols
-    )
-    mixed_rows = lax.all_to_all(mixed, "tensor", split_axis=1, concat_axis=2, tiled=True)
-
     row_count = samples * seq_len // ways
     run = min(row_count, seq_len)
     images = row_count // run
+
+    def rows_of(device):
+        start = lax.rem(device * row_count, seq_len) if run < seq_len else 0
+        if run < seq_len and run % 128 == 0:
+            start = pl.multiple_of(start, 128)
+        return pl.ds(device * row_count // seq_len, images), pl.ds(start, run)
+
+    def take_tokens(ref, device):
+        which, rows = rows_of(device)
+        return ref.at[:, which, :, rows] if run < seq_len else ref.at[:, which]
+
+    mixed = jnp.concatenate([student_mixed, teacher_mixed], axis=0).reshape(
+        3, samples, head_cols, seq_len
+    )
+    (mixed_rows,) = exchange(
+        "tensor",
+        0,
+        [mixed],
+        [(ways, 3, images, head_cols, run)],
+        [(take_tokens, block_of)],
+    )
     first = me * row_count // seq_len
     own_gate = lax.dynamic_slice_in_dim(gate, first, images, axis=1)
     own_strength = lax.dynamic_slice_in_dim(strength, first, images, axis=0)[:, None]
-    student_proj = jnp.dot(mixed_rows[0], student_out_full, preferred_element_type=jnp.float32)
+    mixed_rows = mixed_rows.transpose(1, 2, 0, 3, 4).reshape(3, images, model_width, run)
+    student_proj = jnp.einsum(
+        "ier,ed->ird", mixed_rows[0], student_out_full, preferred_element_type=jnp.float32
+    )
     teacher_proj = jnp.einsum(
-        "kre,ed->krd", mixed_rows[1:], teacher_out_full, preferred_element_type=jnp.float32
-    ).reshape(2, images, run, model_width)
-    student_proj = student_proj.reshape(images, run, model_width)
+        "kier,ed->kird", mixed_rows[1:], teacher_out_full, preferred_element_type=jnp.float32
+    )
     scale_norm = 1.0 / math.sqrt(batch_size * seq_len)
     cotangent = scale_norm * (
         own_gate[0][:, None] * student_proj
@@ -224,39 +314,75 @@
         + (own_strength * own_gate[2])[:, None] * teacher_proj[1]
     )
     own_grad_gate = jnp.sum(cotangent * student_proj, axis=1)
-    grad_proj = (
-        (cotangent * own_gate[0][:, None]).astype(jnp.bfloat16).reshape(row_count, model_width)
-    )
-    grad_mixed_rows = lax.dot_general(
-        grad_proj, student_out_full, (((1,), (1,)), ((), ())), preferred_element_type=jnp.float32
+    grad_proj = (cotangent * own_gate[0][:, None]).astype(jnp.bfloat16)
+    grad_mixed_rows = (
+        jnp.einsum("ed,ird->eir", student_out_full, grad_proj, preferred_element_type=jnp.float32)
+        .astype(jnp.bfloat16)
+        .reshape(ways, head_cols, images, run)
+        .transpose(0, 2, 1, 3)
+    )
+
+    def put_heads(ref, device):
+        which, rows = rows_of(device)
+        return ref.at[which, :, rows] if run < seq_len else ref.at[which]
+
+    (grad_low,) = exchange(
+        "tensor",
+        1,
+        [grad_mixed_rows],
+        [(samples, head_cols, seq_len)],
+        [(block_of, put_heads)],
+    )
+    grad_low = grad_low.reshape(samples, heads_here, HD, seq_len)
+    late_proj, grad_low = lax.optimization_barrier((grad_proj, grad_low))
+    grad_out_part = jnp.einsum(
+        "ier,ird->ed", mixed_rows[0], late_proj, preferred_element_type=jnp.float32
     ).astype(jnp.bfloat16)
-    grad_low = lax.all_to_all(grad_mixed_rows, "tensor", split_axis=1, concat_axis=0, tiled=True)
-    grad_low = grad_low.reshape(samples, seq_len, heads_here, HD)
-    grad_out_part = lax.dot_general(
-        mixed_rows[0], grad_proj, (((0,), (0,)), ((), ())), preferred_element_type=jnp.float32
-    ).astype(jnp.bfloat16)
-    grad_out = lax.psum_scatter(grad_out_part, "tensor", scatter_dimension=0, tiled=True)
-    grad_out = lax.psum_scatter(grad_out, "dp", scatter_dimension=1, tiled=True).astype(jnp.float32)
+    grad_out_rows = lax.psum_scatter(grad_out_part, "tensor", scatter_dimension=0, tiled=True)
 
     grad_qkv_act = attend_grad(heads_qkv, attn_prob, prob_low, grad_low)
-    grad_qkv_t, grad_mod = weight_grad(normed, grad_qkv_act, scale[0], shift[0], student_qkv.T)
-    grad_qkv = lax.psum_scatter(
-        grad_qkv_t.T.astype(jnp.bfloat16), "dp", scatter_dimension=0, tiled=True
-    ).astype(jnp.float32)
-
+    grad_qkv_part, grad_mod = weight_grad(
+        normed, grad_qkv_act, scale[0], shift[0], student_qkv.T
+    )
     grad_gate = lax.dynamic_update_slice_in_dim(
         jnp.zeros((samples, model_width), jnp.float32), own_grad_gate, first, axis=0
     )
-    grad_mod = jnp.concatenate([grad_mod, grad_gate[:, None]], axis=1)
-    act_all = lax.all_gather(student_act, "dp", axis=0, tiled=True)
-    wide_grad = lax.psum_scatter(grad_mod, "tensor", scatter_dimension=2, tiled=True)
-    wide_grad = lax.all_gather(wide_grad, "dp", axis=0, tiled=True)
-    act_cols = model_width // groups
-    own_act = lax.dynamic_slice_in_dim(act_all, lax.axis_index("dp") * act_cols, act_cols, axis=1)
+    grad_mod = jnp.concatenate([grad_mod, grad_gate[:, None]], axis=1).reshape(
+        samples * 3, ways, width_part
+    )
+    (mod_terms,) = exchange(
+        "tensor",
+        2,
+        [grad_mod.transpose(1, 0, 2)],
+        [(ways, samples * 3, width_part)],
+        [(block_of, block_of)],
+    )
+    own_mod = jnp.sum(mod_terms, axis=0)
+    depth = model_width // groups
+    qkv_terms, out_terms, wide_grad, act_all = exchange(
+        "dp",
+        3,
+        [
+            grad_qkv_part.reshape(groups, depth, head_cols * 3),
+            grad_out_rows.reshape(head_cols, groups, depth).transpose(1, 0, 2),
+            own_mod,
+            student_act,
+        ],
+        [
+            (groups, depth, head_cols * 3),
+            (groups, head_cols, depth),
+            (groups, samples * 3, width_part),
+            (groups, samples, model_width),
+        ],
+        [(block_of, block_of), (block_of, block_of), (whole_of, block_of), (whole_of, block_of)],
+    )
+    grad_qkv = jnp.sum(qkv_terms.astype(jnp.float32), axis=0)
+    grad_out = jnp.sum(out_terms.astype(jnp.float32), axis=0)
+    own_act = lax.dynamic_slice_in_dim(act_all, lax.axis_index("dp") * depth, depth, axis=2)
     grad_ada = jnp.einsum(
         "bd,bke->kde",
-        own_act.astype(jnp.float32),
-        wide_grad,
+        own_act.reshape(batch_size, depth).astype(jnp.float32),
+        wide_grad.reshape(batch_size, 3, width_part),
         precision=lax.Precision.HIGHEST,
     )
     return (grad_qkv, grad_out, grad_ada)

time: 380 us -> 301 us (0.79)
  waiting for transfers between devices: 157 us -> 29.4 us
  Pallas kernels: 7.87 us -> 123 us
  local copies, waits for them, and re-layouts: 72.2 us -> 27.3 us
  blocking collectives: 37.1 us -> 20.1 us
  other arithmetic: 20.4 us -> 28.6 us
  starting transfers between devices: 7.41 us -> 0.16 us
  matrix products: 61 us -> 56.5 us
    pallas_call x0 -> x4, Pallas kernels: none -> 114 us  [exchange(): pl.pallas_call(functools.partial(exchange_kernel, axis, slots, count), ou...]
    all_to_all x2 -> x0, waiting for transfers between devices: 64.8 us -> none  [the longest x1 38.6 us: local(): lax.all_to_all(mixed, 'tensor', split_axis=1, concat_axis=2, tiled=True)]
    unnamed x10 -> x4, waiting for transfers between devices: 61.7 us -> 1.41 us
    unnamed x49 -> x41, local copies, waits for them, and re-layouts: 38.2 us -> 6.68 us
    all_gather x2 -> x0, blocking collectives: 17 us -> none  [the longest x1 8.64 us: local(): wide_grad = lax.all_gather(wide_grad, 'dp', axis=0, tiled=True)]
    reshape x4 -> x5, local copies, waits for them, and re-layouts: 13.3 us -> 4.02 us  [the longest x2 2.19 us: local(): grad_out_rows.reshape(head_cols, groups, depth).transpose(1, 0, 2)]
    all_to_all x2 -> x0, starting transfers between devices: 7.13 us -> none  [the longest x1 3.59 us: local(): lax.all_to_all(mixed, 'tensor', split_axis=1, concat_axis=2, tiled=True)]
    reduce_sum x0 -> x3, other arithmetic: none -> 5.67 us  [the longest x1 2.33 us: local(): grad_qkv = jnp.sum(qkv_terms.astype(jnp.float32), axis=0)]
  transfers between devices with their start and end apart: 9 -> 4, of which waited for: 6 -> 1; matrix products, arithmetic and copies ran while one was open for 37% -> 29% of each run, Pallas kernels for 2% -> 24%
where the time goes in v2:
time: 301 us; the launch traced here: 300 us
  Pallas kernels  123 us (41%)
  matrix products  56.5 us (19%)
  waiting for transfers between devices  29.4 us (10%)
  other arithmetic  28.6 us (10%)
  local copies, waits for them, and re-layouts  27.3 us (9%)
  blocking collectives  20.1 us (7%)
  between operations  15 us (5%)
    pallas_call x4, Pallas kernels, exchange(): pl.pallas_call(functools.partial(exchange_kernel, axis, slots, count), ou...  114 us
    all_gather x1, waiting for transfers between devices, local(): wide_noisy = lax.all_gather(noisy, 'tensor', axis=2, tiled=True)  27.9 us
    all_gather x1, blocking collectives, gather_mods(): gathered = lax.all_gather(mods, 'tensor', axis=0)  20.1 us
    sub x2, other arithmetic, attend(): exponent = jnp.exp(scores - jnp.max(scores, axis=-1, keepdims=True))  9.56 us
    dot_general x2, matrix products, project_qkv(): jnp.einsum('bld,df->blf', full_rows, qkv_weight, preferred_element_type=j...  9.12 us
    pallas_call x1, Pallas kernels, weight_grad(): pl.pallas_call(weight_grad_kernel, grid=(samples,), in_specs=[pl.BlockSpe...  8.08 us
    dot_general x1, matrix products, attend_grad(): jnp.einsum('bhlm,bmhe->blhe', grad_scores, key_rows, preferred_element_ty...  7.61 us
    dot_general x1, matrix products, attend_grad(): jnp.einsum('bhlm,blhe->bmhe', grad_scores, queries, preferred_element_typ...  7.52 us
  transfers between devices with their start and end apart: 4, of which 1 were waited for; matrix products, arithmetic and copies ran while one was open for 29% of the time, Pallas kernels for 24%

profile of v2, /device:TPU:0, one launch (start us, length us, event | category | flops | bytes accessed | tf_op | source)
XLA Modules:
  0.0 299.5 jit_solution(14737493195651390234)
XLA Ops:
  7.3 2.2 copy.107
  9.5 0.7 all-gather.8.cloned.1.call-update
  10.3 0.7 all-gather.6.cloned.1.call-update
  11.1 0.8 convert_reduce_fusion.3
  11.9 1.1 multiply_convert_fusion.3
  13.0 2.1 multiply_convert_fusion.4
  15.2 0.2 multiply_convert_fusion.5.refs_3_
  15.4 0.4 convolution_bitcast_fusion.2
  15.9 0.4 convolution_bitcast_fusion.1
  16.3 20.1 %all_gather.13 = f32[8,72,144]{2,1,0:T(8,128)S(1)} all-gather(f32[1,72,144]{2,1,0:T(8,128)S(1)} %bitcast.154), channel_id=1, replica_groups=mesh['dp'=4,'tensor'=8] {'tensor'}, dimensions={0}, use_global_device_ids=true | all-gather | bytes 373248 | tf_op jit(solution)/shard_map/all_gather | solution.py:392
  36.5 0.1 add.140
  36.6 0.1 add.141
  36.7 0.1 add.145
  37.2 0.2 select_reduce_fusion
  37.5 0.1 squeeze.39
  37.6 0.6 dynamic_slice.10
  38.9 0.7 dynamic-slice_reduce_fusion
  39.6 27.9 %all-gather.4.cloned.1.call-done = bf16[8,256,1152]{1,0,2:T(8,128)(2,1)} async-done(((bf16[8,256,144]{1,0,2:T(8,128)(2,1)}), bf16[8,256,1152]{1,0,2:T(8,128)(2,1)}) %all-gather.4.cloned.1.call-update) | async-done | bytes 4718608 | tf_op jit(solution)/shard_map/all_gather | solution.py:230
  67.5 7.0 %copy.108 = bf16[8,256,1152]{2,1,0:T(8,128)(2,1)} copy(bf16[8,256,1152]{1,0,2:T(8,128)(2,1)} %all-gather.4.cloned.1.call-done) | data formatting | bytes 9437184 | tf_op jit(solution)/shard_map/all_gather | solution.py:230
  74.6 4.1 %convert_reduce_fusion = (f32[8,256]{1,0:T(8,128)S(1)}, f32[8,256]{1,0:T(8,128)S(1)}) fusion(bf16[8,256,1152]{2,1,0:T(8,128)(2,1)} %copy.108), kind=kLoop, calls=%fused_computation.8 | loop fusion | flops 9433088 | bytes 4734976 | tf_op jit(solution)/shard_map/reduce_sum | solution.py:259
  78.7 1.3 fusion.4.act_ref
  80.0 2.6 fusion.46
  82.6 0.8 fusion.73
  83.4 4.5 %fusion.9 = (bf16[8,256,1152]{2,1,0:T(8,128)(2,1)S(1)}, bf16[8,256,1152]{2,1,0:T(8,128)(2,1)}) fusion(bf16[8,256,1152]{2,1,0:T(8,128)(2,1)S(1)} %fusion.4.act_ref, f32[8,1152]{1,0:T(8,128)S(1)} %add.141, f32[8,1152]{1,0:T(8,128)S(1)} %add.140, f32[8,1152]{1,0:T(8,128)S(1)} %add.146, f32[8,1152]{1,0:T(8,128)S(1)} %add.145), kind=kLoop, calls=%fused_computation.15 | loop fusion | flops 16515072 | bytes 14303232 | tf_op jit(solution)/shard_map/convert_element_type | solution.py:133
  87.9 3.2 %fusion.100 = (f32[8,2,256]{2,1,0:T(2,128)S(1)}, f32[8,2,256,256]{2,3,1,0:T(8,128)}) fusion(f32[8,2,256,256]{2,3,1,0:T(8,128)S(1)} %fusion.73), kind=kOutput, calls=%fused_computation.136 | output fusion | flops 4194559 | bytes 8404992 | tf_op jit(solution)/shard_map/sub | solution.py:35
  91.2 0.9 copy-done.16
  92.1 6.6 %fusion.40 = bf16[16,256,432]{1,2,0:T(8,128)(2,1)} fusion(bf16[8,256,1152]{2,1,0:T(8,128)(2,1)S(1)} %copy-done.7, bf16[8,256,1152]{2,1,0:T(8,128)(2,1)S(1)} %get-tuple-element.26, bf16[1152,432]{0,1:T(8,128)(2,1)S(1)} %copy-done.16), kind=kOutput, calls=%fused_computation.44 | convolution fusion | flops 4083351552 | bytes 13971456 | tf_op jit(solution)/shard_map/bld,df->blf/dot_general | solution.py:139
  98.6 3.1 %fusion.67 = f32[16,2,256,256]{2,3,1,0:T(8,128)S(1)} fusion(bf16[16,256,2,3,72]{1,4,3,2,0:T(8,128)(2,1)} %bitcast.149), kind=kOutput, calls=%fused_computation.71 | convolution fusion | flops 301989888 | bytes 10747904 | tf_op jit(solution)/shard_map/blhe,bmhe->bhlm/dot_general | solution.py:32
  101.7 0.5 convolution_convert_fusion.3
  102.3 6.3 %fusion.99 = (f32[16,2,256]{2,1,0:T(2,128)S(1)}, f32[16,2,256,256]{2,3,1,0:T(8,128)S(1)}) fusion(f32[16,2,256,256]{2,3,1,0:T(8,128)S(1)} %fusion.67), kind=kOutput, calls=%fused_computation.135 | output fusion | flops 8388863 | bytes 16809984 | tf_op jit(solution)/shard_map/sub | solution.py:35
  108.6 2.2 fusion.49
  110.8 1.4 pad_maximum_fusion
  112.2 50.6 %shard_map.157 = bf16[8,3,1,144,256]{4,3,2,1,0:T(8,128)(2,1)} custom-call(bf16[3,8,144,256]{3,2,1,0:T(8,128)(2,1)} %bitcast.131), custom_call_target="tpu_custom_call" | custom-call | bytes 40000000 | tf_op jit(solution)/shard_map/pallas_call | solution.py:109
  162.8 1.4 slice.126
  164.2 1.1 slice.125
  165.4 5.1 %fusion.31 = f32[2,256,1152]{2,1,0:T(8,128)} fusion(bf16[2,1152,256]{2,1,0:T(8,128)(2,1)S(1)} %bitcast.135, bf16[1152,1152]{1,0:T(8,128)(2,1)} %all-gather.8.cloned.1.call-done), kind=kOutput, calls=%fused_computation.38 | convolution fusion | flops 1358954496 | bytes 6193152 | tf_op jit(solution)/shard_map/kier,ed->kird/dot_general | solution.py:307
  170.5 3.8 %multiply_reduce_fusion.3 = (f32[1152]{0:T(1024)S(1)}, f32[256,1152]{1,0:T(8,128)S(1)}) fusion(f32[2,256,1152]{2,1,0:T(8,128)} %fusion.31, f32[1152]{0:T(1024)S(1)} %get-tuple-element.23, f32[1152]{0:T(1024)S(1)} %get-tuple-element.22, f32[1152]{0:T(1024)S(1)} %get-tuple-element.21, bf16[1152,256]{1,0:T(8,128)(2,1)S(1)} %bitcast.136, ...), kind=kOutput, calls=%fused_computation.74 | convolution fusion | flops 681835392 | bytes 6801408 | tf_op jit(solution)/shard_map/ier,ed->ird/dot_general | solution.py:304
  174.4 1.1 fusion.39
  175.4 1.1 copy.126
  176.5 25.7 %shard_map.158 = bf16[8,144,256]{2,1,0:T(8,128)(2,1)} custom-call(bf16[8,1,144,256]{3,2,1,0:T(8,128)(2,1)} %bitcast.140), custom_call_target="tpu_custom_call" | custom-call | bytes 40000000 | tf_op jit(solution)/shard_map/pallas_call | solution.py:109
  202.2 2.4 convolution_convert_fusion
  204.7 0.1 broadcast_in_dim_squeeze.5.shift_ref
  204.8 0.1 broadcast_in_dim_squeeze.4.scale_ref
  205.0 3.8 %fusion.74 = f32[8,2,256,256]{2,3,1,0:T(8,128)} fusion(bf16[8,2,72,256]{3,2,1,0:T(8,128)(2,1)S(1)} %bitcast.141, bf16[8,256,2,3,72]{1,4,3,2,0:T(8,128)(2,1)} %bitcast.146), kind=kOutput, calls=%fused_computation.88 | convolution fusion | flops 150994944 | bytes 5373952 | tf_op jit(solution)/shard_map/bhel,bmhe->bhlm/dot_general | solution.py:50
  208.8 7.6 %fusion.60 = bf16[8,256,2,1,72]{1,4,2,0,3:T(8,128)(2,1)S(1)} fusion(f32[8,2,256,256]{2,3,1,0:T(8,128)} %fusion.74, bf16[8,256,2,3,72]{1,4,3,2,0:T(8,128)(2,1)} %bitcast.147, f32[8,2,256,256]{2,3,1,0:T(8,128)} %get-tuple-element.44, f32[8,2,256]{2,1,0:T(2,128)S(1)} %get-tuple-element.43), kind=kOutput, calls=%fused_computation.63 | convolution fusion | flops 158634240 | bytes 17989632 | tf_op jit(solution)/shard_map/bhlm,bmhe->blhe/dot_general | solution.py:55
  216.4 7.5 %fusion.57 = bf16[8,256,2,1,72]{1,4,2,0,3:T(8,128)(2,1)S(1)} fusion(f32[8,2,256,256]{2,3,1,0:T(8,128)} %fusion.74, bf16[8,256,2,3,72]{1,4,3,2,0:T(8,128)(2,1)} %bitcast.148, f32[8,2,256,256]{2,3,1,0:T(8,128)} %get-tuple-element.44, f32[8,2,256]{2,1,0:T(2,128)S(1)} %get-tuple-element.43), kind=kOutput, calls=%fused_computation.62 | convolution fusion | flops 158634240 | bytes 17989632 | tf_op jit(solution)/shard_map/bhlm,blhe->bmhe/dot_general | solution.py:58
  224.0 3.0 %fusion.56 = bf16[8,256,2,1,72]{1,4,2,0,3:T(8,128)(2,1)S(1)} fusion(bf16[8,2,72,256]{3,2,1,0:T(8,128)(2,1)S(1)} %bitcast.142, f32[8,2,256,256]{2,3,1,0:T(8,128)} %get-tuple-element.44, f32[8,2,256]{2,1,0:T(2,128)S(1)} %get-tuple-element.43), kind=kOutput, calls=%fused_computation.61 | convolution fusion | flops 153387008 | bytes 5390336 | tf_op jit(solution)/shard_map/bhlm,bhel->bmhe/dot_general | solution.py:61
  227.0 0.2 pad_maximum_fusion.1
  227.2 1.3 copy.130
  228.5 2.8 copy.133.grad_ref
  231.3 2.4 copy-done.3
  233.7 8.1 %shard_map.159 = (bf16[1152,432]{1,0:T(8,128)(2,1)S(1)}, f32[8,2,1152]{2,1,0:T(2,128)S(1)}) custom-call(bf16[8,256,1152]{2,1,0:T(8,128)(2,1)S(1)} %copy-done.3, bf16[8,256,432]{2,1,0:T(8,128)(2,1)S(1)} %copy.133.grad_ref, f32[8,1,1152]{2,1,0:T(1,128)S(1)} %broadcast_in_dim_squeeze.4.scale_ref, f32[8,1,1152]{2,1,0:T(1,128)S(1)} %broadcast_in_dim_squeeze.5.shift_ref, ...), custom_call_target="tpu_custom_call" | custom-call | flops 2038431744 | bytes 9474048 | tf_op jit(solution)/shard_map/pallas_call | solution.py:178
  241.8 1.0 copy-done.4
  243.0 0.2 reshape.192
  243.1 0.7 copy.154
  243.9 11.9 %shard_map.160 = f32[8,24,144]{2,1,0:T(8,128)} custom-call(f32[8,24,144]{2,1,0:T(8,128)} %bitcast.152), custom_call_target="tpu_custom_call" | custom-call | bytes 40000000 | tf_op jit(solution)/shard_map/pallas_call | solution.py:109
  255.8 1.6 reduce_sum.97.refs_2_
  257.3 1.4 reshape.191
  258.7 0.8 copy.153
  259.5 26.3 %shard_map.161 = (bf16[4,288,432]{2,1,0:T(8,128)(2,1)}, bf16[4,144,288]{2,1,0:T(8,128)(2,1)}, f32[4,24,144]{2,1,0:T(8,128)}, bf16[4,8,1152]{2,1,0:T(8,128)(2,1)}) custom-call(bf16[4,288,432]{2,1,0:T(8,128)(2,1)} %bitcast.129, bf16[4,144,288]{2,1,0:T(8,128)(2,1)} %bitcast.143, f32[24,144]{1,0:T(8,128)} %reduce_sum.97.refs_2_, bf16[8,1152]{1,0:T(8,128)(2,1)} %copy-done.13), custom_call_target="tpu_custom_call" | custom-call | bytes 40000000 | tf_op jit(solution)/shard_map/pallas_call | solution.py:109
  285.8 0.9 reshape.193
  286.8 2.3 convert_reduce_fusion.1
  289.1 1.8 convert_reduce_fusion.2
  290.9 2.1 convolution_bitcast_fusion
  (67 shorter events, 1.2 us)
Async XLA Ops:
  7.2 4.7 %copy-start = (bf16[1000,1152]{1,0:T(8,128)(2,1)S(1)}, bf16[1000,1152]{1,0:T(8,128)(2,1)}, u32[]{:S(2)}) copy-start(bf16[1000,1152]{1,0:T(8,128)(2,1)} %param.19) | copy-start | bytes 6912004
  7.2 5.8 %copy-start.14 = (s32[8]{0:T(128)S(1)}, s32[8]{0:T(128)}, u32[]{:S(2)}) copy-start(s32[8]{0:T(128)} %param.15) | copy-start | bytes 100
  7.2 8.0 %copy-start.18 = (s32[8]{0:T(128)S(1)}, s32[8]{0:T(128)}, u32[]{:S(2)}) copy-start(s32[8]{0:T(128)} %param.17) | copy-start | bytes 100
  7.2 8.0 %copy-start.17 = (bf16[32,1152]{1,0:T(8,128)(2,1)S(1)}, bf16[32,1152]{1,0:T(8,128)(2,1)}, u32[]{:S(2)}) copy-start(bf16[32,1152]{1,0:T(8,128)(2,1)} %param.20) | copy-start | bytes 221188
  7.2 8.7 %copy-start.11 = (bf16[3,1152,144]{1,2,0:T(8,128)(2,1)S(1)}, bf16[3,1152,144]{1,2,0:T(8,128)(2,1)}, u32[]{:S(2)}) copy-start(bf16[3,1152,144]{1,2,0:T(8,128)(2,1)} %param.24) | copy-start | bytes 2985988
  7.2 60.3 %all-gather.4.cloned.1.call-start = ((), (), s32[]{:S(2)}) async-start(), calls=%async_computation.1 | async-start | bytes 5308416 | tf_op jit(solution)/shard_map/all_gather | solution.py:230
  9.5 155.9 %all-gather.8.cloned.1.call-start = ((), (), s32[]{:S(2)}) async-start(), calls=%async_computation.3 | async-start | bytes 2985984 | tf_op jit(solution)/shard_map/all_gather | solution.py:255
  10.3 160.2 %all-gather.6.cloned.1.call-start = ((), (), s32[]{:S(2)}) async-start(), calls=%async_computation.2 | async-start | bytes 2985984 | tf_op jit(solution)/shard_map/all_gather | solution.py:256
  11.0 246.4 %reduce-scatter.2.cloned.1.call-start = ((), (), s32[]{:S(2)}) async-start(), calls=%async_computation.4 | async-start | bytes 2985984 | tf_op jit(solution)/shard_map/reduce_scatter | solution.py:341
  11.1 4.4 %copy-start.12 = (bf16[3,1152,144]{1,2,0:T(8,128)(2,1)S(1)}, bf16[3,1152,144]{1,2,0:T(8,128)(2,1)}, u32[]{:S(2)}) copy-start(bf16[3,1152,144]{1,2,0:T(8,128)(2,1)} %param.27) | copy-start | bytes 2985988
  13.0 24.2 %copy-start.19 = (f32[32]{0:T(128)S(1)}, f32[32]{0:T(128)}, u32[]{:S(2)}) copy-start(f32[32]{0:T(128)} %param.21) | copy-start | bytes 388
  15.4 59.1 %copy-start.13 = (bf16[8,1152]{1,0:T(8,128)(2,1)}, bf16[8,1152]{1,0:T(8,128)(2,1)S(1)}, u32[]{:S(2)}) copy-start(bf16[8,1152]{1,0:T(8,128)(2,1)S(1)} %multiply_convert_fusion.5.refs_3_) | copy-start | bytes 55300
  74.6 4.2 %copy-start.6 = (bf16[8,256,1152]{2,1,0:T(8,128)(2,1)S(1)}, bf16[8,256,1152]{2,1,0:T(8,128)(2,1)}, u32[]{:S(2)}) copy-start(bf16[8,256,1152]{2,1,0:T(8,128)(2,1)} %copy.108) | copy-start | bytes 14155780
  78.7 1.3 copy-start.5
  80.0 3.3 %copy-start.2 = (bf16[8,256,1152]{2,1,0:T(8,128)(2,1)}, bf16[8,256,1152]{2,1,0:T(8,128)(2,1)S(1)}, u32[]{:S(2)}) copy-start(bf16[8,256,1152]{2,1,0:T(8,128)(2,1)S(1)} %fusion.4.act_ref) | copy-start | bytes 14155780
  82.6 19.1 %copy-start.10 = (bf16[8,256,432]{1,2,0:T(8,128)(2,1)}, bf16[8,256,432]{1,2,0:T(8,128)(2,1)S(1)}, u32[]{:S(2)}) copy-start(bf16[8,256,432]{1,2,0:T(8,128)(2,1)S(1)} %fusion.46) | copy-start | bytes 5308420
  87.9 3.3 %copy-start.7 = (bf16[8,256,1152]{2,1,0:T(8,128)(2,1)S(1)}, bf16[8,256,1152]{2,1,0:T(8,128)(2,1)}, u32[]{:S(2)}) copy-start(bf16[8,256,1152]{2,1,0:T(8,128)(2,1)} %get-tuple-element.27) | copy-start | bytes 14155780
  87.9 4.2 %copy-start.16 = (bf16[1152,432]{0,1:T(8,128)(2,1)S(1)}, bf16[1152,432]{0,1:T(8,128)(2,1)}, u32[]{:S(2)}) copy-start(bf16[1152,432]{0,1:T(8,128)(2,1)} %param.22) | copy-start | bytes 2985988
  98.6 3.1 %copy-start.8 = (f32[8,2,256,256]{2,3,1,0:T(8,128)S(1)}, f32[8,2,256,256]{2,3,1,0:T(8,128)}, u32[]{:S(2)}) copy-start(f32[8,2,256,256]{2,3,1,0:T(8,128)} %get-tuple-element.44) | copy-start | bytes 12582916
  170.5 3.9 %copy-start.15 = (bf16[1152,1152]{1,0:T(8,128)(2,1)S(1)}, bf16[1152,1152]{1,0:T(8,128)(2,1)}, u32[]{:S(2)}) copy-start(bf16[1152,1152]{1,0:T(8,128)(2,1)} %all-gather.6.cloned.1.call-done) | copy-start | bytes 7962628
  202.2 2.7 copy-start.9
  231.3 2.4 copy-start.3
  241.8 1.0 copy-start.4
  242.9 50.1 %copy-start.1 = (bf16[1000,1152]{1,0:T(8,128)(2,1)S(1)}, bf16[1000,1152]{1,0:T(8,128)(2,1)}, u32[]{:S(2)}) copy-start(bf16[1000,1152]{1,0:T(8,128)(2,1)} %param.19) | copy-start | bytes 6912004
Sparse Core Ops, SparseCore 0:
  10.2 57.2 all-gather.3
  69.1 33.6 all-gather.7
  104.5 61.5 all-gather.5
  204.8 41.4 reduce-scatter.1
